TPU v7x, 256 devices: a whole 4x4x8 slice. The times are simulated.
256 devices in a mesh: atom: 32 (over y_lo, z, core), band: 8 (over y_hi, x).
Axes of the slice: x: 4, y: 4 (y_hi: 2, y_lo: 2; y = y_hi * 2 + y_lo), z: 8, core: 2. Of those that a mesh axis runs over, the one named last changes fastest.
Arguments:
- wave_rows: bfloat16 [512, 65536], P('atom', 'band'), may hold values from -6 to 6
- projectors: bfloat16 [4096, 65536], P('atom', 'band'), may hold values from -0.0234375 to 0.0234375
- dij_table: float32 [16, 8, 8], replicated, may hold values from -6 to 6
- dij_index: int32 [512], P('atom'), may hold values from 0 to 15
- proj_count: int32 [512], P('atom'), may hold values from 1 to 8
Outputs:
- nonlocal_rows: bfloat16 [512, 65536], P('atom', 'band')
All inputs are finite; a program needn't handle non-finite values.
Results may differ from a plain program's by a relative error of at most 0.0049.
Values may be sent and summed in bfloat16 or wider, within the bound.
A program may use at most 128 MiB of HBM per device.

v0:
```python
import jax
import jax.numpy as jnp
from jax import lax
from jax.sharding import Mesh
from jax.sharding import PartitionSpec as P

ATOM = ("atom_0", "atom_1", "atom_2")


def cut_along(shard, dim, count):
    before, after = (shard.shape[:dim], shard.shape[dim + 1 :])
    return jnp.moveaxis(shard.reshape(*before, count, -1, *after), dim, 0)


def sum_at_owner(shard, axis, dim):
    count = lax.axis_size(axis)
    blocks = lax.all_to_all(cut_along(shard, dim, count), axis, 0, 0, tiled=True)
    return jnp.sum(blocks, axis=0)


def sent_to_all(shard, axis):
    count = lax.axis_size(axis)
    return lax.all_to_all(
        jnp.broadcast_to(shard[None], (count, *shard.shape)), axis, 0, 0, tiled=True
    )


def in_order(blocks, dim):
    blocks = jnp.moveaxis(blocks, 0, dim)
    lengths = blocks.shape
    return blocks.reshape(*lengths[:dim], lengths[dim] * lengths[dim + 1], *lengths[dim + 2 :])


def gathered_copies(shard, axis, dim):
    blocks = sent_to_all(shard, axis)
    return in_order(blocks, dim)


def scatter_pairs(shard, chips, core, dim):
    sizes = (lax.axis_size(chips), lax.axis_size(core))
    blocks = cut_along(shard, dim, sizes[0] * sizes[1])
    inside = blocks.shape[1:]
    blocks = blocks.reshape(*sizes, *inside).swapaxes(0, 1).reshape(-1, *inside)
    blocks = lax.psum_scatter(blocks, core, scatter_dimension=0, tiled=True)
    return lax.psum_scatter(blocks, chips, scatter_dimension=0, tiled=True)[0]


def shards(wave_rows, projectors, dij_table, dij_index, proj_count):
    atom_local = dij_index.shape[0]
    kind_total = dij_table.shape[0]
    per_atom = dij_table.shape[1]
    width = atom_local * per_atom
    partial_value = lax.dot_general(
        lax.all_gather(wave_rows, ATOM, axis=0, tiled=True),
        projectors,
        (((1,), (1,)), ((), ())),
        preferred_element_type=jnp.float32,
    )
    kind_onehot = (dij_index[:, None] == jnp.arange(kind_total, dtype=jnp.int32)[None, :]).astype(
        jnp.float32
    )
    blocks = jnp.dot(
        kind_onehot,
        dij_table.reshape(kind_total, per_atom * per_atom),
        precision=lax.Precision.HIGHEST,
    ).reshape(atom_local, per_atom, per_atom)
    active = (jnp.arange(per_atom, dtype=jnp.int32)[None, :] < proj_count[:, None]).astype(
        jnp.float32
    )
    blocks = blocks * active[:, :, None] * active[:, None, :]
    share = sum_at_owner(partial_value, "band", 0)
    count = share.shape[0]
    mixed = jnp.einsum(
        "baj,aij->bai",
        share.reshape(count, atom_local, per_atom),
        blocks,
        precision=lax.Precision.HIGHEST,
    )
    weighted = gathered_copies(mixed.reshape(count, width).astype(jnp.bfloat16), "band", 0)
    result = scatter_pairs(
        jnp.dot(weighted, projectors, preferred_element_type=jnp.float32),
        ("atom_0", "atom_1"),
        "atom_2",
        0,
    )
    return result.astype(jnp.bfloat16)


def solution(mesh):
    split = Mesh(
        mesh.devices.reshape(2, 8, 2, mesh.shape["band"]), ("atom_0", "atom_1", "atom_2", "band")
    )
    return jax.shard_map(
        shards,
        mesh=split,
        in_specs=(P(ATOM, "band"), P(ATOM, "band"), P(), P(ATOM), P(ATOM)),
        out_specs=P(ATOM, "band"),
        check_vma=False,
    )
```

profile of v0, /device:TPU:8, one launch (start us, length us, event | category | flops | bytes accessed | tf_op | source)
XLA Modules:
  0.0 264.0 jit_solution(16585991134371336601)
XLA Ops:
  6.5 0.0 copy-start
  6.5 0.0 copy-start.3
  6.5 0.0 copy-start.2
  6.5 0.0 copy-start.1
  6.5 0.0 all-gather.2.cloned.1.call-start
  6.6 0.7 all-gather.2.cloned.1.call-update
  7.3 76.4 %all-gather.2.cloned.1.call-done = bf16[512,8192]{1,0:T(8,128)(2,1)} async-done(((bf16[16,8192]{1,0:T(8,128)(2,1)}), bf16[512,8192]{1,0:T(8,128)(2,1)}) %all-gather.2.cloned.1.call-update) | async-done | bytes 8388624 | tf_op jit(solution)/shard_map/all_gather | solution.py:54
  83.7 0.0 copy-done
  83.7 6.4 %fusion.9 = f32[512,128]{1,0:T(8,128)} fusion(bf16[512,8192]{1,0:T(8,128)(2,1)} %all-gather.2.cloned.1.call-done, bf16[128,8192]{1,0:T(8,128)(2,1)S(1)} %copy-done), kind=kOutput, calls=%fused_computation.14 | convolution fusion | flops 1073741824 | bytes 10747904 | tf_op jit(solution)/shard_map/dot_general | solution.py:53
  90.1 5.9 %all-to-all-start = ((f32[8,64,128]{2,1,0:T(8,128)}), f32[8,64,128]{2,1,0:T(8,128)S(1)}, u32[]{:S(2)}, u32[]{:S(2)}) async-start(f32[8,64,128]{2,1,0:T(8,128)} %bitcast.4), calls=%async_computation | async-start | bytes 524288 | tf_op jit(solution)/shard_map/all_to_all | solution.py:17
  96.0 0.0 reduce-scatter.3.cloned.1.call-start
  96.0 0.0 copy-done.3
  96.1 0.0 copy-done.2
  96.1 0.0 copy-done.1
  96.1 0.2 fusion.2
  96.3 0.1 copy.14
  96.4 8.8 %all-to-all-done = f32[8,64,128]{2,1,0:T(8,128)S(1)} async-done(((f32[8,64,128]{2,1,0:T(8,128)}), f32[8,64,128]{2,1,0:T(8,128)S(1)}, u32[]{:S(2)}, u32[]{:S(2)}) %all-to-all-start) | async-done | bytes 262176 | tf_op jit(solution)/shard_map/all_to_all | solution.py:17
  105.2 0.1 copy.13
  105.3 0.3 fusion.1
  105.6 0.1 copy.15
  105.7 10.6 %all_to_all.10 = bf16[8,64,128]{2,1,0:T(8,128)(2,1)S(1)} all-to-all(bf16[8,64,128]{2,1,0:T(8,128)(2,1)S(1)} %broadcast_in_dim.2), channel_id=1, replica_groups=mesh['atom_0'=2,'atom_1'=8,'atom_2'=2,'band'=8] {'band'}, dimensions={0} | all-to-all | bytes 262144 | tf_op jit(solution)/shard_map/all_to_all | solution.py:23
  116.3 2.3 convolution_bitcast_fusion
  118.6 6.0 %copy.16 = f32[2,16,16,8192]{3,2,1,0:T(8,128)} copy(f32[2,16,16,8192]{3,2,0,1:T(8,128)S(1)} %convolution_bitcast_fusion) | data formatting | bytes 33554432 | tf_op jit(solution)/shard_map/transpose | solution.py:43
  124.7 0.0 reduce-scatter.3.cloned.1.call-update
  124.7 0.0 reduce-scatter.5.cloned.1.call-start
  124.8 26.8 %reduce-scatter.3.cloned.1.call-done = f32[16,16,8192]{2,1,0:T(8,128)} async-done(((f32[32,16,8192]{2,1,0:T(8,128)}), f32[16,16,8192]{2,1,0:T(8,128)}) %reduce-scatter.3.cloned.1.call-update) | async-done | bytes 8388624 | tf_op jit(solution)/shard_map/reduce_scatter | solution.py:44
  151.6 0.0 reduce-scatter.5.cloned.1.call-update
  151.6 104.1 %reduce-scatter.5.cloned.1.call-done = f32[1,16,8192]{2,1,0:T(8,128)} async-done(((f32[16,16,8192]{2,1,0:T(8,128)}), f32[1,16,8192]{2,1,0:T(8,128)}) %reduce-scatter.5.cloned.1.call-update) | async-done | bytes 524304 | tf_op jit(solution)/shard_map/reduce_scatter | solution.py:45
  255.7 1.8 convert_bitcast_fusion
  (3 shorter events, 0.1 us)
Async XLA Ops:
  6.5 77.1 %copy-start = (bf16[128,8192]{1,0:T(8,128)(2,1)S(1)}, bf16[128,8192]{1,0:T(8,128)(2,1)}, u32[]{:S(2)}) copy-start(bf16[128,8192]{1,0:T(8,128)(2,1)} %param.6) | copy-start | bytes 6291460
  6.5 89.5 %copy-start.3 = (s32[16]{0:T(128)S(1)}, s32[16]{0:T(128)}, u32[]{:S(2)}) copy-start(s32[16]{0:T(128)} %param.9) | copy-start | bytes 196
  6.5 89.5 %copy-start.2 = (s32[16]{0:T(128)S(1)}, s32[16]{0:T(128)}, u32[]{:S(2)}) copy-start(s32[16]{0:T(128)} %param.8) | copy-start | bytes 196
  6.5 89.5 %copy-start.1 = (f32[16,8,8]{0,2,1:T(8,128)S(1)}, f32[16,8,8]{0,2,1:T(8,128)}, u32[]{:S(2)}) copy-start(f32[16,8,8]{0,2,1:T(8,128)} %param.7) | copy-start | bytes 12292
  6.5 77.1 %all-gather.2.cloned.1.call-start = ((), (), s32[]{:S(2)}) async-start(), calls=%async_computation.4 | async-start | bytes 8650752 | tf_op jit(solution)/shard_map/all_gather | solution.py:54
  90.1 15.1 %all-to-all-start = ((f32[8,64,128]{2,1,0:T(8,128)}), f32[8,64,128]{2,1,0:T(8,128)S(1)}, u32[]{:S(2)}, u32[]{:S(2)}) async-start(f32[8,64,128]{2,1,0:T(8,128)} %bitcast.4), calls=%async_computation | async-start | bytes 524288 | tf_op jit(solution)/shard_map/all_to_all | solution.py:17
  96.0 55.6 %reduce-scatter.3.cloned.1.call-start = ((), (), s32[]{:S(2)}) async-start(), calls=%async_computation.5 | async-start | bytes 25165824 | tf_op jit(solution)/shard_map/reduce_scatter | solution.py:44
  124.7 131.0 %reduce-scatter.5.cloned.1.call-start = ((), (), s32[]{:S(2)}) async-start(), calls=%async_computation.6 | async-start | bytes 8912896 | tf_op jit(solution)/shard_map/reduce_scatter | solution.py:45
Sparse Core Ops, SparseCore 0:
  9.2 74.4 all-gather.1
  124.8 26.7 reduce-scatter.2
  154.2 101.5 reduce-scatter.4
where the time goes:
time: 266 us; the launch traced here: 264 us
  waiting for transfers between devices  217 us (82%)
  between operations  13.2 us (5%)
  blocking collectives  10.6 us (4%)
  matrix products  9.22 us (3%)
  local copies, waits for them, and re-layouts  6.35 us (2%)
  starting transfers between devices  6.04 us (2%)
    reduce_scatter x1, waiting for transfers between devices, scatter_pairs(): return lax.psum_scatter(blocks, chips, scatter_dimension=0, tiled=True)[0]  104 us
    all_gather x1, waiting for transfers between devices, shards(): lax.all_gather(wave_rows, ATOM, axis=0, tiled=True)  76.4 us
    reduce_scatter x1, waiting for transfers between devices, scatter_pairs(): blocks = lax.psum_scatter(blocks, core, scatter_dimension=0, tiled=True)  26.8 us
    all_to_all x1, blocking collectives, sent_to_all(): lax.all_to_all(jnp.broadcast_to(shard[None], (count, *shard.shape)), axis...  10.6 us
    all_to_all x1, waiting for transfers between devices, sum_at_owner(): lax.all_to_all(cut_along(shard, dim, count), axis, 0, 0, tiled=True)  8.77 us
    dot_general x1, matrix products, shards(): lax.dot_general(lax.all_gather(wave_rows, ATOM, axis=0, tiled=True), proj...  6.41 us
    transpose x1, local copies, waits for them, and re-layouts, scatter_pairs(): blocks = blocks.reshape(*sizes, *inside).swapaxes(0, 1).reshape(-1, *inside)  6.05 us
    all_to_all x1, starting transfers between devices, sum_at_owner(): lax.all_to_all(cut_along(shard, dim, count), axis, 0, 0, tiled=True)  5.93 us
  transfers between devices with their start and end apart: 4, of which 4 were waited for; matrix products, arithmetic and copies ran while one was open for 0% of the time, Pallas kernels for 0%

commit v1 on v0

v1 whole, which is shorter than its diff:
```python
import functools

import jax
import jax.numpy as jnp
from jax import lax
from jax.experimental import pallas as pl
from jax.experimental.pallas import tpu as pltpu
from jax.sharding import PartitionSpec as P

MESH = pl.DeviceIdType.MESH
F32 = jnp.float32
BF16 = jnp.bfloat16
Z = 8
SIDE = 4
PLANE = SIDE * SIDE
PIECES = 4
UP, DOWN = 0, 1
STEPS = {(0, UP): 4, (0, DOWN): 3, (1, UP): 3, (1, DOWN): 4}
RING = [(t, k, d) for t in range(4) for k in (0, 1) for d in (UP, DOWN) if t < STEPS[k, d]]


def kernel(
    wave_ref, proj_ref, coef_ref, out_ref,
    bands, away, proj, coefs, part, parts, weighted, result, sent, came, final, mix,
    ring_send, ring_recv, y_send, y_recv, c_send, c_recv, piece_send, piece_recv, pass_send, pass_recv,
    part_send, part_recv, wt_send, wt_recv, sum_send, sum_recv, local_sem,
):
    rows, half = away.shape
    count = coef_ref.shape[1]
    atom, band = lax.axis_index("atom"), lax.axis_index("band")
    y_lo, z, core = atom // (2 * Z), (atom // 2) % Z, atom % 2
    y_hi, x = band // SIDE, band % SIDE
    y = y_hi * 2 + y_lo
    me = y * SIDE + x
    slot = y_lo * 2 + core

    def at(lo, zz, cc, hi=y_hi, xx=x):
        return (lo * (2 * Z) + zz * 2 + cc, hi * SIDE + xx)

    mate = at(y_lo, z, 1 - core)
    across = at(1 - y_lo, z, core)
    corner = at(1 - y_lo, z, 1 - core)
    z_next = (at(y_lo, (z + 1) % Z, core), at(y_lo, (z + Z - 1) % Z, core))
    shifts = [(dy, dx) for dy in range(SIDE) for dx in range(SIDE) if dy or dx]

    def plane(dy, dx):
        yy, xx = (y + dy) % SIDE, (x + dx) % SIDE
        return yy * SIDE + xx, at(yy % 2, z, core, yy // 2, xx)

    def remote(src, dst, send, recv, to):
        return pltpu.make_async_remote_copy(
            src_ref=src, dst_ref=dst, send_sem=send, recv_sem=recv, device_id=to, device_id_type=MESH
        )

    mine = pl.ds(pl.multiple_of(y_lo * half, half), half)
    theirs = pl.ds(pl.multiple_of((1 - y_lo) * half, half), half)

    own_bands = pltpu.make_async_copy(wave_ref.at[:, mine], bands.at[z * 2 + y_lo], local_sem.at[0])
    away_bands = pltpu.make_async_copy(wave_ref.at[:, theirs], away, local_sem.at[1])
    own_proj = pltpu.make_async_copy(proj_ref.at[:, mine], proj.at[slot], local_sem.at[2])
    own_coefs = pltpu.make_async_copy(coef_ref, coefs.at[slot], local_sem.at[3])
    for copy in (own_bands, away_bands, own_coefs, own_proj):
        copy.start()

    barrier = pltpu.get_barrier_semaphore()
    greet = [mate, corner, *z_next] + [plane(*s)[1] for s in shifts]
    for to in greet:
        pl.semaphore_signal(barrier, inc=1, device_id=to, device_id_type=MESH)
    pl.semaphore_wait(barrier, len(greet))

    started = []

    def go(copy):
        copy.start()
        started.append(copy)

    def ring_copy(k, d, t):
        source = (z + Z - t) % Z if d == UP else (z + t) % Z
        index = source * 2 + (y_lo if k == 0 else 1 - y_lo)
        return remote(bands.at[index], bands.at[index], ring_send.at[k, d, t], ring_recv.at[k, d, t], z_next[d])

    away_bands.wait()
    y_bands = remote(away, bands.at[z * 2 + y_lo], y_send.at[0], y_recv.at[0], across)
    go(y_bands)
    own_bands.wait()
    for d in (UP, DOWN):
        go(ring_copy(0, d, 0))
    own_coefs.wait()
    coef_copies = [
        remote(coefs.at[slot], coefs.at[slot], c_send.at[i], c_recv.at[i], to) for i, to in enumerate((mate, across, corner))
    ]
    for copy in coef_copies:
        go(copy)
    size = count // PIECES
    pieces = [
        remote(
            proj_ref.at[pl.ds(i * size, size), theirs],
            proj.at[slot, pl.ds(i * size, size), :],
            piece_send.at[i], piece_recv.at[i], across,
        )
        for i in range(PIECES)
    ]
    for copy in pieces:
        go(copy)
    own_proj.wait()
    to_mate = remote(proj.at[slot], proj.at[slot], y_send.at[1], y_recv.at[1], mate)
    go(to_mate)

    y_bands.wait_recv()
    for d in (UP, DOWN):
        go(ring_copy(1, d, 0))
    far = (1 - y_lo) * 2 + core
    passed = []
    for t in range(4):
        for k in (0, 1):
            for d in (UP, DOWN):
                if t < STEPS[k, d]:
                    ring_copy(k, d, t).wait_recv()
                    if t + 1 < STEPS[k, d]:
                        go(ring_copy(k, d, t + 1))
        pieces[t].wait_recv()
        block = proj.at[far, pl.ds(t * size, size), :]
        passing = remote(block, block, pass_send.at[t], pass_recv.at[t], mate)
        go(passing)
        passed.append(passing)

    for copy in coef_copies:
        copy.wait_recv()
    same = lax.broadcasted_iota(jnp.int32, (128, 128), 0) // 8 == lax.broadcasted_iota(jnp.int32, (128, 128), 1) // 8
    for s in range(4):
        mix[s] = jnp.where(same, jnp.concatenate([coefs[s]] * 16, axis=0), 0.0)
    to_mate.wait_recv()
    for copy in passed:
        copy.wait_recv()

    every = PLANE * rows

    @pl.loop(0, 2)
    def _(n):
        value = lax.dot_general(
            bands[...].reshape(every, half),
            proj[pl.ds(n * 2, 2)].reshape(2 * count, half),
            (((1,), (1,)), ((), ())),
            preferred_element_type=F32,
        )
        part[:, :, pl.ds(pl.multiple_of(n * 2 * count, 2 * count), 2 * count)] = value.reshape(PLANE, rows, 2 * count)

    part_copies = []
    for i, s in enumerate(shifts):
        chunk, to = plane(*s)
        part_copies.append(remote(part.at[chunk], parts.at[i], part_send.at[i], part_recv.at[i], to))
        go(part_copies[-1])
    total = part[me]
    for i, copy in enumerate(part_copies):
        copy.wait_recv()
        total += parts[i]
    mixed = [
        jnp.dot(
            total[:, s * count : (s + 1) * count], mix[s], precision=lax.Precision.HIGHEST, preferred_element_type=F32
        )
        for s in range(4)
    ]
    weighted[me] = jnp.concatenate(mixed, axis=1).astype(BF16)
    wt_copies = []
    for i, s in enumerate(shifts):
        _, to = plane(*s)
        wt_copies.append(remote(weighted.at[me], weighted.at[me], wt_send.at[i], wt_recv.at[i], to))
        go(wt_copies[-1])
    for copy in wt_copies:
        copy.wait_recv()

    tile = 512

    @pl.loop(0, half // tile)
    def _(n):
        columns = pl.ds(pl.multiple_of(n * tile, tile), tile)
        value = jnp.dot(
            weighted[...].reshape(every, 4 * count),
            proj[:, :, columns].reshape(4 * count, tile),
            preferred_element_type=F32,
        )
        result[:, :, columns] = value.reshape(PLANE, rows, tile)

    width = half // 2

    def own_sum(owner, k):
        return result[pl.ds(owner * 2, 2), :, pl.ds(k * width, width)]

    def sum_copy(k, d, t):
        return remote(sent.at[k, d, t], came.at[k, d, t], sum_send.at[k, d, t], sum_recv.at[k, d, t], z_next[d])

    for t in range(5):
        for k in (0, 1):
            for d in (UP, DOWN):
                n = STEPS[k, d]
                if t < n:
                    owner = (z + (n - t)) % Z if d == UP else (z + Z - (n - t)) % Z
                    value = own_sum(owner, k)
                    if t > 0:
                        sum_copy(k, d, t - 1).wait_recv()
                        value += came[k, d, t - 1].astype(F32)
                    sent[k, d, t] = value.astype(BF16)
                    go(sum_copy(k, d, t))
    ends = []
    outs = []
    for k in (0, 1):
        value = own_sum(z, k)
        for d in (UP, DOWN):
            last = STEPS[k, d] - 1
            sum_copy(k, d, last).wait_recv()
            value += came[k, d, last].astype(F32)
        final[:, :, k * width : (k + 1) * width] = value.astype(BF16)
        columns = pl.ds(pl.multiple_of(y_lo * half + k * width, width), width)
        there = remote(
            final.at[1 - y_lo, :, pl.ds(k * width, width)], out_ref.at[:, columns], y_send.at[2 + k], y_recv.at[2 + k], across
        )
        go(there)
        ends.append(there)
        here = pltpu.make_async_copy(
            final.at[y_lo, :, pl.ds(k * width, width)], out_ref.at[:, columns], local_sem.at[4 + k]
        )
        here.start()
        outs.append(here)
    for copy in ends:
        copy.wait_recv()
    for copy in outs:
        copy.wait()
    for copy in started:
        copy.wait_send()


def shards(wave_rows, projectors, dij_table, dij_index, proj_count):
    rows, width = wave_rows.shape
    count = projectors.shape[0]
    half = width // 2
    kinds, per_atom, _ = dij_table.shape
    index = jnp.repeat(dij_index, per_atom)
    acting = jnp.repeat(proj_count, per_atom)
    place = jnp.arange(count, dtype=jnp.int32) % per_atom
    spread = jnp.tile(jnp.transpose(dij_table, (0, 2, 1)), (1, 1, count // per_atom))
    chosen = jnp.where(index[None, None, :] == jnp.arange(kinds, dtype=jnp.int32)[:, None, None], spread, 0.0)
    coefs = jnp.sum(chosen, axis=0)
    rows_on = jnp.arange(per_atom, dtype=jnp.int32)[:, None] < acting[None, :]
    coefs = jnp.where(rows_on & (place < acting)[None, :], coefs, 0.0)

    dma = pltpu.SemaphoreType.DMA
    others = PLANE - 1
    return pl.pallas_call(
        kernel,
        out_shape=jax.ShapeDtypeStruct((rows, width), BF16),
        in_specs=[pl.BlockSpec(memory_space=pl.ANY)] * 3,
        out_specs=pl.BlockSpec(memory_space=pl.ANY),
        scratch_shapes=[
            pltpu.VMEM((PLANE, rows, half), BF16),
            pltpu.VMEM((rows, half), BF16),
            pltpu.VMEM((4, count, half), BF16),
            pltpu.VMEM((4, per_atom, count), F32),
            pltpu.VMEM((PLANE, rows, 4 * count), F32),
            pltpu.VMEM((others, rows, 4 * count), F32),
            pltpu.VMEM((PLANE, rows, 4 * count), BF16),
            pltpu.VMEM((PLANE, rows, half), F32),
            pltpu.VMEM((2, 2, 4, 2, rows, half // 2), BF16),
            pltpu.VMEM((2, 2, 4, 2, rows, half // 2), BF16),
            pltpu.VMEM((2, rows, half), BF16),
            pltpu.VMEM((4, count, count), F32),
            dma((2, 2, 4)), dma((2, 2, 4)),
            dma((4,)), dma((4,)),
            dma((3,)), dma((3,)),
            dma((PIECES,)), dma((PIECES,)),
            dma((PIECES,)), dma((PIECES,)),
            dma((others,)), dma((others,)),
            dma((others,)), dma((others,)),
            dma((2, 2, 4)), dma((2, 2, 4)),
            dma((6,)),
        ],
        compiler_params=pltpu.CompilerParams(
            collective_id=0, has_side_effects=True, vmem_limit_bytes=48 * 1024 * 1024
        ),
        name="nonlocal_rows",
    )(wave_rows, projectors, coefs)


def solution(mesh):
    return jax.shard_map(
        shards,
        mesh=mesh,
        in_specs=(P("atom", "band"), P("atom", "band"), P(), P("atom"), P("atom")),
        out_specs=P("atom", "band"),
        check_vma=False,
    )
```

time: 266 us -> 90.7 us (0.34)
  waiting for transfers between devices: 217 us -> 0 us
  Pallas kernels: 0 us -> 83.9 us
  between operations: 13.2 us -> 0.06 us
  blocking collectives: 10.6 us -> 0 us
  matrix products: 9.22 us -> 0 us
  starting transfers between devices: 6.04 us -> 0 us
    reduce_scatter x2 -> x0, waiting for transfers between devices: 131 us -> none  [the longest x1 104 us: scatter_pairs(): return lax.psum_scatter(blocks, chips, scatter_dimension=0, tiled=True)[0]]
    pallas_call x0 -> x1, Pallas kernels: none -> 83.9 us  [shards(): pl.pallas_call(kernel, out_shape=jax.ShapeDtypeStruct((rows, width), BF16...]
    all_gather x1 -> x0, waiting for transfers between devices: 76.4 us -> none  [shards(): lax.all_gather(wave_rows, ATOM, axis=0, tiled=True)]
    all_to_all x1 -> x0, blocking collectives: 10.6 us -> none  [sent_to_all(): lax.all_to_all(jnp.broadcast_to(shard[None], (count, *shard.shape)), axis...]
    dot_general x4 -> x0, matrix products: 9.22 us -> none  [the longest x1 6.41 us: shards(): lax.dot_general(lax.all_gather(wave_rows, ATOM, axis=0, tiled=True), proj...]
    all_to_all x1 -> x0, waiting for transfers between devices: 8.77 us -> none  [sum_at_owner(): lax.all_to_all(cut_along(shard, dim, count), axis, 0, 0, tiled=True)]
    all_to_all x1 -> x0, starting transfers between devices: 5.93 us -> none  [sum_at_owner(): lax.all_to_all(cut_along(shard, dim, count), axis, 0, 0, tiled=True)]
    transpose x1, local copies, waits for them, and re-layouts: 6.05 us -> 0.85 us  [shards(): jnp.transpose(dij_table, (0, 2, 1))]
  transfers between devices with their start and end apart: 4 -> 0, of which waited for: 4 -> 0; matrix products, arithmetic and copies ran while one was open for 0% -> 0% of each run, Pallas kernels for 0% -> 0%
where the time goes in v1:
time: 90.7 us; the launch traced here: 89.9 us
  Pallas kernels  83.9 us (93%)
  local copies, waits for them, and re-layouts  5.07 us (6%)
    pallas_call x1, Pallas kernels, shards(): pl.pallas_call(kernel, out_shape=jax.ShapeDtypeStruct((rows, width), BF16...  83.9 us
    unnamed x5, local copies, waits for them, and re-layouts  3.24 us

profile of v1, /device:TPU:8, one launch (start us, length us, event | category | flops | bytes accessed | tf_op | source)
XLA Modules:
  0.0 89.9 jit_solution(11244064654717105805)
XLA Ops:
  0.0 0.7 broadcast_in_dim.23
  0.7 0.1 lt.29
  0.8 0.7 iota_compare_fusion
  1.5 0.8 copy.8
  2.4 0.2 select_reduce_fusion
  2.6 0.1 copy.9
  2.6 0.1 reduce_sum.12
  2.8 0.0 copy-start
  2.8 1.6 %copy-done = bf16[128,8192]{1,0:T(8,128)(2,1)S(1)} copy-done((bf16[128,8192]{1,0:T(8,128)(2,1)S(1)}, bf16[128,8192]{1,0:T(8,128)(2,1)}, u32[]{:S(2)}) %copy-start) | copy-done | bytes 2097176
  4.3 0.0 copy-start.1
  4.3 0.9 %copy-done.1 = bf16[16,8192]{1,0:T(8,128)(2,1)S(1)} copy-done((bf16[16,8192]{1,0:T(8,128)(2,1)S(1)}, bf16[16,8192]{1,0:T(8,128)(2,1)}, u32[]{:S(2)}) %copy-start.1) | copy-done | bytes 262168
  5.3 83.9 %nonlocal_rows.1 = bf16[16,8192]{1,0:T(8,128)(2,1)S(1)} custom-call(bf16[16,8192]{1,0:T(8,128)(2,1)S(1)} %copy-done.1, bf16[128,8192]{1,0:T(8,128)(2,1)S(1)} %copy-done, f32[8,128]{1,0:T(8,128)S(1)} %fusion.1.coef_ref), custom_call_target="tpu_custom_call" | custom-call | tf_op jit(solution)/shard_map/nonlocal_rows/pallas_call | solution.py:248
  89.2 0.7 copy.11
  (2 shorter events, 0.0 us)
Async XLA Ops:
  2.8 1.6 %copy-start = (bf16[128,8192]{1,0:T(8,128)(2,1)S(1)}, bf16[128,8192]{1,0:T(8,128)(2,1)}, u32[]{:S(2)}) copy-start(bf16[128,8192]{1,0:T(8,128)(2,1)} %proj_ref.1) | copy-start | bytes 6291460
  4.3 0.9 %copy-start.1 = (bf16[16,8192]{1,0:T(8,128)(2,1)S(1)}, bf16[16,8192]{1,0:T(8,128)(2,1)}, u32[]{:S(2)}) copy-start(bf16[16,8192]{1,0:T(8,128)(2,1)} %wave_ref.1) | copy-start | bytes 786436

commit v2 on v1

v2 whole, which is shorter than its diff:
```python
import functools

import jax
import jax.numpy as jnp
from jax import lax
from jax.experimental import pallas as pl
from jax.experimental.pallas import tpu as pltpu
from jax.sharding import PartitionSpec as P

MESH = pl.DeviceIdType.MESH
F32 = jnp.float32
BF16 = jnp.bfloat16
scope = jax.named_scope
Z = 8
SIDE = 4
PLANE = SIDE * SIDE
PIECES = 4
UP, DOWN = 0, 1
STEPS = ((4, 3), (3, 4))


def kernel(
    wave_ref, proj_ref, table_ref, index_ref, count_ref, out_ref,
    bands, away, proj, table, index, acting, coefs, part, parts, weighted, result, sent, came, final, mix,
    ring_send, ring_recv, y_send, y_recv, c_send, c_recv, piece_send, piece_recv, pass_send, pass_recv,
    part_send, part_recv, wt_send, wt_recv, sum_send, sum_recv, end_send, end_recv, local_sem,
):
    rows, half = away.shape
    count = proj.shape[1]
    per_atom, _, kinds = table.shape
    share = rows // 2
    atom, band = lax.axis_index("atom"), lax.axis_index("band")
    y_lo, z, core = atom // (2 * Z), (atom // 2) % Z, atom % 2
    y_hi, x = band // SIDE, band % SIDE
    y = y_hi * 2 + y_lo
    me = y * SIDE + x
    slot = y_lo * 2 + core

    def at(lo, zz, cc, hi=y_hi, xx=x):
        return (lo * (2 * Z) + zz * 2 + cc, hi * SIDE + xx)

    mate = at(y_lo, z, 1 - core)
    across = at(1 - y_lo, z, core)
    corner = at(1 - y_lo, z, 1 - core)
    z_next = (at(y_lo, (z + 1) % Z, core), at(y_lo, (z + Z - 1) % Z, core))
    shifts = [(dy, dx) for dy in range(SIDE) for dx in range(SIDE) if dy or dx]

    def plane(dy, dx):
        yy, xx = (y + dy) % SIDE, (x + dx) % SIDE
        return yy * SIDE + xx, at(yy % 2, z, core, yy // 2, xx)

    def remote(src, dst, send, recv, to):
        return pltpu.make_async_remote_copy(
            src_ref=src, dst_ref=dst, send_sem=send, recv_sem=recv, device_id=to, device_id_type=MESH
        )

    mine = pl.ds(pl.multiple_of(y_lo * half, half), half)
    theirs = pl.ds(pl.multiple_of((1 - y_lo) * half, half), half)

    away_bands = pltpu.make_async_copy(wave_ref.at[:, theirs], away, local_sem.at[0])
    own_bands = pltpu.make_async_copy(wave_ref.at[:, mine], bands.at[y_lo, z], local_sem.at[1])
    own_proj = pltpu.make_async_copy(proj_ref.at[:, mine], proj.at[slot], local_sem.at[2])
    small = [
        pltpu.make_async_copy(table_ref, table, local_sem.at[3]),
        pltpu.make_async_copy(index_ref, index, local_sem.at[4]),
        pltpu.make_async_copy(count_ref, acting, local_sem.at[5]),
    ]
    for copy in (away_bands, own_bands, own_proj, *small):
        copy.start()

    barrier = pltpu.get_barrier_semaphore()
    greet = [mate, corner, *z_next] + [plane(*s)[1] for s in shifts]
    for to in greet:
        pl.semaphore_signal(barrier, inc=1, device_id=to, device_id_type=MESH)
    with scope("barrier"):
        pl.semaphore_wait(barrier, len(greet))

    started = []

    def go(copy):
        copy.start()
        started.append(copy)
        return copy

    def ring_copy(k, d, t):
        source = (z + Z - t) % Z if d == UP else (z + t) % Z
        block = bands.at[y_lo if k == 0 else 1 - y_lo, source]
        return remote(block, block, ring_send.at[k, d, t], ring_recv.at[k, d, t], z_next[d])

    away_bands.wait()
    y_bands = go(remote(away, bands.at[y_lo, z], y_send.at[0], y_recv.at[0], across))
    own_bands.wait()
    for d in (UP, DOWN):
        go(ring_copy(0, d, 0))
    size = count // PIECES
    pieces = [
        go(
            remote(
                proj_ref.at[pl.ds(i * size, size), theirs],
                proj.at[slot, pl.ds(i * size, size), :],
                piece_send.at[i], piece_recv.at[i], across,
            )
        )
        for i in range(PIECES)
    ]
    own_proj.wait()
    to_mate = go(remote(proj.at[slot], proj.at[slot], y_send.at[1], y_recv.at[1], mate))

    for copy in small:
        copy.wait()
    wide = (per_atom, count)
    lane = lax.broadcasted_iota(jnp.int32, wide, 1)
    inner = lane % per_atom
    chosen = jnp.zeros(wide, jnp.int32)
    limit = jnp.zeros(wide, jnp.int32)
    for a in range(count // per_atom):
        chosen = jnp.where(lane // per_atom == a, index[a], chosen)
        limit = jnp.where(lane // per_atom == a, acting[a], limit)
    kind = lax.broadcasted_iota(jnp.int32, (kinds, count), 0)
    value = jnp.zeros(wide, F32)
    for i in range(per_atom):
        pick = jnp.where((kind == chosen[:1]) & (inner[:1] == i), 1.0, 0.0).astype(F32)
        value += jnp.dot(table[i], pick, precision=lax.Precision.HIGHEST, preferred_element_type=F32)
    on = (inner < limit) & (lax.broadcasted_iota(jnp.int32, wide, 0) < limit)
    coefs[slot] = jnp.where(on, value, 0.0)

    with scope("ybands"):
        y_bands.wait_recv()
    for d in (UP, DOWN):
        go(ring_copy(1, d, 0))
    coef_copies = [
        go(remote(coefs.at[slot], coefs.at[slot], c_send.at[i], c_recv.at[i], to))
        for i, to in enumerate((mate, across, corner))
    ]
    far = (1 - y_lo) * 2 + core
    passed = []
    for t in range(4):
        for k in (0, 1):
            for d in (UP, DOWN):
                if t < STEPS[k][d]:
                    with scope(f"ag{t}{k}{d}"):
                        ring_copy(k, d, t).wait_recv()
                    if t + 1 < STEPS[k][d]:
                        go(ring_copy(k, d, t + 1))
        with scope(f"piece{t}"):
            pieces[t].wait_recv()
        block = proj.at[far, pl.ds(t * size, size), :]
        passed.append(go(remote(block, block, pass_send.at[t], pass_recv.at[t], mate)))

    for copy in coef_copies:
        copy.wait_recv()
    square = (count, count)
    same = lax.broadcasted_iota(jnp.int32, square, 0) // per_atom == lax.broadcasted_iota(jnp.int32, square, 1) // per_atom
    for s in range(4):
        mix[s] = jnp.where(same, jnp.concatenate([coefs[s]] * (count // per_atom), axis=0), 0.0)
    with scope("passed"):
        to_mate.wait_recv()
        for copy in passed:
            copy.wait_recv()

    group = Z * rows
    part_copies = [[], []]
    for g in (0, 1):
        with scope(f"S{g}"):

            @pl.loop(0, 2)
            def _(n):
                value = lax.dot_general(
                    bands[g].reshape(group, half),
                    proj[pl.ds(n * 2, 2)].reshape(2 * count, half),
                    (((1,), (1,)), ((), ())),
                    preferred_element_type=F32,
                )
                columns = pl.ds(pl.multiple_of(n * 2 * count, 2 * count), 2 * count)
                part[g, :, :, columns] = value.reshape(PLANE, share, 2 * count)

        for i, s in enumerate(shifts):
            chunk, to = plane(*s)
            part_copies[g].append(
                go(remote(part.at[g, chunk], parts.at[g, i], part_send.at[g, i], part_recv.at[g, i], to))
            )
    wt_copies = [[], []]
    for g in (0, 1):
        with scope(f"part{g}"):
            for copy in part_copies[g]:
                copy.wait_recv()
        with scope(f"mix{g}"):
            total = part[g, me]
            for i in range(len(shifts)):
                total += parts[g, i]
            mixed = [
                jnp.dot(
                    total[:, s * count : (s + 1) * count], mix[s],
                    precision=lax.Precision.HIGHEST, preferred_element_type=F32,
                )
                for s in range(4)
            ]
            weighted[g, me] = jnp.concatenate(mixed, axis=1).astype(BF16)
        for i, s in enumerate(shifts):
            _, to = plane(*s)
            block = weighted.at[g, me]
            wt_copies[g].append(go(remote(block, block, wt_send.at[g, i], wt_recv.at[g, i], to)))

    tile = 512
    width = half // 2

    def own_sum(g, h, owner):
        return result[g, owner, :, h * width : (h + 1) * width]

    def sum_copy(g, h, d, t):
        return remote(
            sent.at[g, h, d, t], came.at[g, h, d, t], sum_send.at[g, h, d, t], sum_recv.at[g, h, d, t], z_next[d]
        )

    def sum_step(g, h, d, t):
        n = STEPS[h][d]
        owner = (z + (n - t)) % Z if d == UP else (z + Z - (n - t)) % Z
        value = own_sum(g, h, owner)
        if t > 0:
            with scope(f"rs{t - 1}{g}{h}{d}"):
                sum_copy(g, h, d, t - 1).wait_recv()
            value += came[g, h, d, t - 1].astype(F32)
        sent[g, h, d, t] = value.astype(BF16)
        go(sum_copy(g, h, d, t))

    for g in (0, 1):
        with scope(f"wt{g}"):
            for copy in wt_copies[g]:
                copy.wait_recv()
        for h in (0, 1):
            with scope(f"O{g}{h}"):

                @pl.loop(0, width // tile)
                def _(n):
                    columns = pl.ds(pl.multiple_of(h * width + n * tile, tile), tile)
                    value = jnp.dot(
                        weighted[g].reshape(group, 4 * count),
                        proj[:, :, columns].reshape(4 * count, tile),
                        preferred_element_type=F32,
                    )
                    result[g, :, :, columns] = value.reshape(Z, rows, tile)

            for d in (UP, DOWN):
                sum_step(g, h, d, 0)
    for t in range(1, 4):
        for g in (0, 1):
            for h in (0, 1):
                for d in (UP, DOWN):
                    if t < STEPS[h][d]:
                        sum_step(g, h, d, t)
    ends = []
    for g in (0, 1):
        for h in (0, 1):
            value = own_sum(g, h, z)
            for d in (UP, DOWN):
                last = STEPS[h][d] - 1
                with scope(f"rs{last}{g}{h}{d}"):
                    sum_copy(g, h, d, last).wait_recv()
                value += came[g, h, d, last].astype(F32)
            final[g, :, h * width : (h + 1) * width] = value.astype(BF16)
            columns = pl.ds(pl.multiple_of(y_lo * half + h * width, width), width)
            there = remote(
                final.at[g, :, pl.ds(h * width, width)], out_ref.at[:, columns], end_send.at[h], end_recv.at[h], across
            )
            here = pltpu.make_async_copy(
                final.at[g, :, pl.ds(h * width, width)], out_ref.at[:, columns], local_sem.at[6 + h]
            )

            @pl.when(y_lo == g)
            def _():
                here.start()

            @pl.when(y_lo != g)
            def _():
                there.start()

            if g == 0:
                ends.append((there, here))
    with scope("ends"):
        for there, here in ends:
            there.wait_recv()
            here.wait()
    with scope("drain"):
        for there, _ in ends:
            there.wait_send()
        for copy in started:
            copy.wait_send()


def shards(wave_rows, projectors, dij_table, dij_index, proj_count):
    rows, width = wave_rows.shape
    count = projectors.shape[0]
    half = width // 2
    kinds, per_atom, _ = dij_table.shape
    atoms = count // per_atom

    dma = pltpu.SemaphoreType.DMA
    others = PLANE - 1
    hbm = pl.BlockSpec(memory_space=pltpu.MemorySpace.HBM)
    return pl.pallas_call(
        kernel,
        out_shape=jax.ShapeDtypeStruct((rows, width), BF16),
        in_specs=[hbm] * 5,
        out_specs=pl.BlockSpec(memory_space=pl.ANY),
        scratch_shapes=[
            pltpu.VMEM((2, Z, rows, half), BF16),
            pltpu.VMEM((rows, half), BF16),
            pltpu.VMEM((4, count, half), BF16),
            pltpu.VMEM((per_atom, per_atom, kinds), F32),
            pltpu.SMEM((atoms,), jnp.int32),
            pltpu.SMEM((atoms,), jnp.int32),
            pltpu.VMEM((4, per_atom, count), F32),
            pltpu.VMEM((2, PLANE, rows // 2, 4 * count), F32),
            pltpu.VMEM((2, others, rows // 2, 4 * count), F32),
            pltpu.VMEM((2, PLANE, rows // 2, 4 * count), BF16),
            pltpu.VMEM((2, Z, rows, half), F32),
            pltpu.VMEM((2, 2, 2, 4, rows, half // 2), BF16),
            pltpu.VMEM((2, 2, 2, 4, rows, half // 2), BF16),
            pltpu.VMEM((2, rows, half), BF16),
            pltpu.VMEM((4, count, count), F32),
            dma((2, 2, 4)), dma((2, 2, 4)),
            dma((2,)), dma((2,)),
            dma((3,)), dma((3,)),
            dma((PIECES,)), dma((PIECES,)),
            dma((PIECES,)), dma((PIECES,)),
            dma((2, others)), dma((2, others)),
            dma((2, others)), dma((2, others)),
            dma((2, 2, 2, 4)), dma((2, 2, 2, 4)),
            dma((2,)), dma((2,)),
            dma((8,)),
        ],
        compiler_params=pltpu.CompilerParams(
            collective_id=0, has_side_effects=True, vmem_limit_bytes=67_043_328
        ),
        name="nonlocal_rows",
    )(wave_rows, projectors, jnp.transpose(dij_table, (1, 2, 0)), dij_index, proj_count)


def solution(mesh):
    return jax.shard_map(
        shards,
        mesh=mesh,
        in_specs=(P("atom", "band"), P("atom", "band"), P(), P("atom"), P("atom")),
        out_specs=P("atom", "band"),
        check_vma=False,
    )
```

time: 90.7 us -> 82 us (0.904)
  Pallas kernels: 83.9 us -> 80.2 us
  local copies, waits for them, and re-layouts: 5.07 us -> 1.67 us
    pallas_call x1, Pallas kernels: 83.9 us -> 80.2 us  [shards(): pl.pallas_call(kernel, out_shape=jax.ShapeDtypeStruct((rows, width), BF16...]
    unnamed x5 -> x1, local copies, waits for them, and re-layouts: 3.24 us -> 1.67 us
where the time goes in v2:
time: 82 us; the launch traced here: 81.9 us
  Pallas kernels  80.2 us (98%)
  local copies, waits for them, and re-layouts  1.67 us (2%)
    pallas_call x1, Pallas kernels, shards(): pl.pallas_call(kernel, out_shape=jax.ShapeDtypeStruct((rows, width), BF16...  80.2 us
    unnamed x1, local copies, waits for them, and re-layouts  1.67 us

profile of v2, /device:TPU:8, one launch (start us, length us, event | category | flops | bytes accessed | tf_op | source)
XLA Modules:
  0.0 81.9 jit_solution(13050637153663270105)
XLA Ops:
  0.0 80.2 %nonlocal_rows.1 = bf16[16,8192]{1,0:T(8,128)(2,1)} custom-call(bf16[16,8192]{1,0:T(8,128)(2,1)} %wave_ref.1, bf16[128,8192]{1,0:T(8,128)(2,1)} %proj_ref.1, f32[8,8,16]{2,1,0:T(8,128)} %bitcast.1, s32[16]{0:T(128)} %index_ref.1, s32[16]{0:T(128)} %count_ref.1), custom_call_target="tpu_custom_call" | custom-call | tf_op jit(solution)/shard_map/nonlocal_rows/pallas_call | solution.py:300
  80.2 1.7 %copy.7 = bf16[16,8192]{1,0:T(8,128)(2,1)} copy(bf16[16,8192]{1,0:T(8,128)(2,1)} %nonlocal_rows.1) | data formatting | bytes 524288

commit v3 on v2

v3 whole, which is shorter than its diff:
```python
import functools

import jax
import jax.numpy as jnp
from jax import lax
from jax.experimental import pallas as pl
from jax.experimental.pallas import tpu as pltpu
from jax.sharding import PartitionSpec as P

MESH = pl.DeviceIdType.MESH
F32 = jnp.float32
BF16 = jnp.bfloat16
scope = jax.named_scope
Z = 8
SIDE = 4
PLANE = SIDE * SIDE
WIDTHS = (1024, 1024, 896, 896, 256)
PARTS = len(WIDTHS)
ALONE = 256
PIECE = 1024
UP, DOWN = 0, 1
RING, ACROSS, PIECE_SEND, MATE, COEFS, PASS, PART, WEIGHTED, SUM, SWAP, END = range(11)
SENDS = 11
STEPS = ((4, 3), (3, 4), (4, 3), (3, 4), (3, 4))


def kernel(
    wave_ref, proj_ref, table_ref, index_ref, count_ref, out_ref,
    bands, away, proj, table, index, acting, coefs, part, parts, weighted, result, sent, came, swap_out, swap_in, final, mix,
    send_sem, ring_recv, y_recv, mate_recv, c_recv, piece_recv, pass_recv, part_recv, wt_recv, sum_recv, swap_recv, end_recv,
    local_sem,
):
    rows, wide = away.shape
    half = wide - ALONE
    both = half - ALONE
    count = proj.shape[2]
    per_atom, _, kinds = table.shape
    share = rows // 2
    atom, band = lax.axis_index("atom"), lax.axis_index("band")
    y_lo, z, core = atom // (2 * Z), (atom // 2) % Z, atom % 2
    y_hi, x = band // SIDE, band % SIDE
    y = y_hi * 2 + y_lo
    me = y * SIDE + x
    slot = y_lo * 2 + core

    def at(lo, zz, cc, hi=y_hi, xx=x):
        return (lo * (2 * Z) + zz * 2 + cc, hi * SIDE + xx)

    mate = at(y_lo, z, 1 - core)
    across = at(1 - y_lo, z, core)
    corner = at(1 - y_lo, z, 1 - core)
    z_next = (at(y_lo, (z + 1) % Z, core), at(y_lo, (z + Z - 1) % Z, core))
    shifts = [(dy, dx) for dy in range(SIDE) for dx in range(SIDE) if dy or dx]
    shifts.sort(key=lambda s: -min(s[0], SIDE - s[0]) - min(s[1], SIDE - s[1]))

    def plane(dy, dx):
        yy, xx = (y + dy) % SIDE, (x + dx) % SIDE
        return yy * SIDE + xx, at(yy % 2, z, core, yy // 2, xx)

    def remote(src, dst, send, recv, to):
        return pltpu.make_async_remote_copy(
            src_ref=src, dst_ref=dst, send_sem=send, recv_sem=recv, device_id=to, device_id_type=MESH
        )

    def columns_of(side, first, size):
        return pl.ds(pl.multiple_of(side * half + first, 128), size)

    mine, theirs = columns_of(y_lo, 0, half), columns_of(1 - y_lo, 0, half)
    mine_alone, theirs_alone = columns_of(y_lo, both, ALONE), columns_of(1 - y_lo, both, ALONE)
    body, rest = pl.ds(0, half), pl.ds(half, ALONE)

    away_bands = [
        pltpu.make_async_copy(wave_ref.at[:, theirs], away.at[:, body], local_sem.at[0]),
        pltpu.make_async_copy(wave_ref.at[:, mine_alone], away.at[:, rest], local_sem.at[1]),
    ]
    own_bands = [
        pltpu.make_async_copy(wave_ref.at[:, mine], bands.at[y_lo, z, :, body], local_sem.at[2]),
        pltpu.make_async_copy(wave_ref.at[:, theirs_alone], bands.at[y_lo, z, :, rest], local_sem.at[3]),
    ]
    own_proj = [
        pltpu.make_async_copy(proj_ref.at[:, mine], proj.at[y_lo, core, :, body], local_sem.at[4]),
        pltpu.make_async_copy(proj_ref.at[:, theirs_alone], proj.at[y_lo, core, :, rest], local_sem.at[5]),
    ]
    small = [
        pltpu.make_async_copy(table_ref, table, local_sem.at[6]),
        pltpu.make_async_copy(index_ref, index, local_sem.at[7]),
        pltpu.make_async_copy(count_ref, acting, local_sem.at[8]),
    ]
    for copy in (*away_bands, *own_bands, *own_proj, *small):
        copy.start()

    barrier = pltpu.get_barrier_semaphore()
    greet = [mate, corner, *z_next] + [plane(*s)[1] for s in shifts]
    for to in greet:
        pl.semaphore_signal(barrier, inc=1, device_id=to, device_id_type=MESH)
    with scope("barrier"):
        pl.semaphore_wait(barrier, len(greet))

    def go(copy):
        copy.start()
        return copy

    def sent_all(ref, sem):
        remote(ref, ref, sem, sem, mate).wait_send()

    def got_all(ref, sem):
        remote(ref, ref, sem, sem, mate).wait_recv()

    def ring_copy(k, h, d, t):
        source = (z + Z - t) % Z if d == UP else (z + t) % Z
        block = bands.at[y_lo if k == 0 else 1 - y_lo, source, :, pl.ds(h * (wide // 2), wide // 2)]
        return remote(block, block, send_sem.at[RING], ring_recv.at[k, h, d * STEPS[h][UP] + t], z_next[d])

    for copy in away_bands:
        copy.wait()
    y_bands = []
    for h in (0, 1):
        columns = pl.ds(h * (wide // 2), wide // 2)
        y_bands.append(
            go(remote(away.at[:, columns], bands.at[y_lo, z, :, columns], send_sem.at[ACROSS], y_recv.at[h], across))
        )
    for copy in own_bands:
        copy.wait()
    for h in (0, 1):
        for d in (UP, DOWN):
            go(ring_copy(0, h, d, 0))
    cuts = [(first, min(PIECE, both - first)) for first in range(0, both, PIECE)]
    pieces = [
        remote(
            proj_ref.at[:, columns_of(1 - y_lo, first, size)], proj.at[y_lo, core, :, pl.ds(first, size)],
            send_sem.at[PIECE_SEND], piece_recv.at[i], across,
        )
        for i, (first, size) in enumerate(cuts)
    ]
    for copy in pieces[:2]:
        go(copy)
    for copy in own_proj:
        copy.wait()
    there = proj.at[y_lo, core]
    to_mate = go(remote(there, there, send_sem.at[MATE], mate_recv.at[0], mate))

    for copy in small:
        copy.wait()
    flat = (per_atom, count)
    lane = lax.broadcasted_iota(jnp.int32, flat, 1)
    inner = lane % per_atom
    chosen = jnp.zeros(flat, jnp.int32)
    limit = jnp.zeros(flat, jnp.int32)
    for a in range(count // per_atom):
        chosen = jnp.where(lane // per_atom == a, index[a], chosen)
        limit = jnp.where(lane // per_atom == a, acting[a], limit)
    kind = lax.broadcasted_iota(jnp.int32, (kinds, count), 0)
    value = jnp.zeros(flat, F32)
    for i in range(per_atom):
        pick = jnp.where((kind == chosen[:1]) & (inner[:1] == i), 1.0, 0.0).astype(F32)
        value += jnp.dot(table[i], pick, precision=lax.Precision.HIGHEST, preferred_element_type=F32)
    on = (inner < limit) & (lax.broadcasted_iota(jnp.int32, flat, 0) < limit)
    coefs[slot] = jnp.where(on, value, 0.0)

    coef_copies = [
        go(remote(coefs.at[slot], coefs.at[slot], send_sem.at[COEFS], c_recv.at[i], to))
        for i, to in enumerate((mate, across, corner))
    ]
    for copy in pieces[2:]:
        go(copy)
    for h in (0, 1):
        with scope(f"ybands{h}"):
            y_bands[h].wait_recv()
        for d in (UP, DOWN):
            go(ring_copy(1, h, d, 0))
    passed = []

    def pass_piece(i):
        with scope(f"piece{i}"):
            pieces[i].wait_recv()
        first, size = cuts[i]
        there = proj.at[1 - y_lo, core, :, pl.ds(first, size)]
        passed.append(go(remote(there, there, send_sem.at[PASS], pass_recv.at[i], mate)))

    def contract(lines, kept):
        return lax.dot_general(lines, kept, (((1,), (1,)), ((), ())), preferred_element_type=F32)

    own_pair = pl.ds(pl.multiple_of(y_lo * 2 * count, count), 2 * count)
    far_pair = pl.ds(pl.multiple_of((1 - y_lo) * 2 * count, count), 2 * count)

    def own_parts(sources):
        lines = [bands[:, source].reshape(2 * rows, wide) for source in sources]
        kept = proj[y_lo].reshape(2 * count, wide)
        value = contract(kept, lines[0]).T if len(lines) == 1 else contract(jnp.concatenate(lines, axis=0), kept)
        for i, source in enumerate(sources):
            here = value[i * 2 * rows : (i + 1) * 2 * rows].reshape(2, 2, share, 2 * count)
            part[:, pl.ds(source * 2, 2), :, own_pair] = here

    def send_parts(g, columns):
        for i, s in enumerate(shifts):
            chunk, to = plane(*s)
            go(
                remote(
                    part.at[g, chunk, :, columns], parts.at[g, i, :, columns], send_sem.at[PART], part_recv.at[g], to
                )
            )

    for t in range(4):
        for k in (0, 1):
            for h in (0, 1):
                for d in (UP, DOWN):
                    if t < STEPS[h][d]:
                        with scope(f"ag{t}{k}{h}{d}"):
                            ring_copy(k, h, d, t).wait_recv()
                        if t + 1 < STEPS[h][d]:
                            go(ring_copy(k, h, d, t + 1))
        if t < 3:
            pass_piece(t)
        if t == 0:
            with scope("tomate"):
                to_mate.wait_recv()
            with scope("S00"):
                own_parts([z])
        with scope(f"S{t + 1}"):
            up, down = (z + Z - t - 1) % Z, (z + t + 1) % Z
            own_parts([up, down] if t < 3 else [up])
    send_parts(0, own_pair)
    pass_piece(3)

    every = 2 * Z * rows
    ready = cuts[3][0]
    with scope("passed0"):
        for copy in passed[:3]:
            copy.wait_recv()
    with scope("Sfar0"):
        value = contract(
            bands[:, :, :, :ready].reshape(every, ready), proj[1 - y_lo, :, :, :ready].reshape(2 * count, ready)
        )
        part[:, :, :, far_pair] = value.reshape(2, PLANE, share, 2 * count)
    with scope("mixes"):
        for copy in coef_copies:
            copy.wait_recv()
        square = (count, count)
        down = lax.broadcasted_iota(jnp.int32, square, 0)
        same = down // per_atom == lax.broadcasted_iota(jnp.int32, square, 1) // per_atom
        for s in range(4):
            mix[s] = jnp.where(same, jnp.concatenate([coefs[s]] * (count // per_atom), axis=0), 0.0)
    with scope("passed"):
        passed[3].wait_recv()
    with scope("Sfar1"):
        value = contract(
            bands[:, :, :, ready:both].reshape(every, both - ready),
            proj[1 - y_lo, :, :, ready:both].reshape(2 * count, both - ready),
        )
        part[:, :, :, far_pair] += value.reshape(2, PLANE, share, 2 * count)
    send_parts(0, far_pair)
    send_parts(1, own_pair)
    send_parts(1, far_pair)
    for g in (0, 1):
        with scope(f"part{g}"):
            got_all(parts.at[g], part_recv.at[g])
        with scope(f"mix{g}"):
            total = part[g, me]
            for i in range(len(shifts)):
                total += parts[g, i]
            mixed = [
                jnp.dot(
                    total[:, s * count : (s + 1) * count], mix[s],
                    precision=lax.Precision.HIGHEST, preferred_element_type=F32,
                )
                for s in range(4)
            ]
            weighted[g, me] = jnp.concatenate(mixed, axis=1).astype(BF16)
        for i, s in enumerate(shifts):
            _, to = plane(*s)
            there = weighted.at[g, me]
            go(remote(there, there, send_sem.at[WEIGHTED], wt_recv.at[g], to))

    group = Z * rows
    tile = 512
    starts = [sum(WIDTHS[:h]) for h in range(PARTS)]
    spans = [slice(first, first + size) for first, size in zip(starts, WIDTHS)]

    def own_sum(g, h, owner):
        return result[g, owner, :, spans[h]]

    def at_step(h, d, t):
        return d * STEPS[h][UP] + t

    def sum_copy(g, h, d, t):
        n = at_step(h, d, t)
        size = pl.ds(0, WIDTHS[h])
        return remote(
            sent.at[g, h, n, :, size], came.at[g, h, n, :, size], send_sem.at[SUM], sum_recv.at[g, h, n], z_next[d]
        )

    def arrived(g, h, d, t):
        return came[g, h, at_step(h, d, t), :, : WIDTHS[h]].astype(F32)

    def sum_step(g, h, d, t):
        n = STEPS[h][d]
        owner = (z + (n - t)) % Z if d == UP else (z + Z - (n - t)) % Z
        value = own_sum(g, h, owner)
        if t > 0:
            with scope(f"rs{t - 1}{h}{d}"):
                sum_copy(g, h, d, t - 1).wait_recv()
            value += arrived(g, h, d, t - 1)
        sent[g, h, at_step(h, d, t), :, : WIDTHS[h]] = value.astype(BF16)
        go(sum_copy(g, h, d, t))

    swaps = []
    for g in (0, 1):
        with scope(f"wt{g}"):
            got_all(weighted.at[g, pl.ds(0, PLANE - 1)], wt_recv.at[g])
        with scope(f"alone{g}"):
            value = jnp.dot(
                weighted[g, :, :, own_pair].reshape(group, 2 * count),
                proj[y_lo, :, :, both:].reshape(2 * count, 2 * ALONE),
                preferred_element_type=F32,
            ).reshape(Z, rows, 2 * ALONE)
            result[g, :, :, both:] = value[:, :, :ALONE]
            swap_out[g] = value[:, :, ALONE:].astype(BF16)
            swaps.append(go(remote(swap_out.at[g], swap_in.at[g], send_sem.at[SWAP], swap_recv.at[g], across)))
        for h in range(PARTS - 1):
            with scope(f"O{g}{h}"):
                for first in range(spans[h].start, spans[h].stop, tile):
                    size = min(tile, spans[h].stop - first)
                    value = jnp.dot(
                        weighted[g].reshape(group, 4 * count),
                        proj[:, :, :, first : first + size].reshape(4 * count, size),
                        preferred_element_type=F32,
                    )
                    result[g, :, :, first : first + size] = value.reshape(Z, rows, size)
            for d in (UP, DOWN):
                sum_step(g, h, d, 0)
    tail = PARTS - 1
    order = [(g, h, t) for g in (0, 1) for h, t in [(tail, 0)] + [(h, 1) for h in range(tail)]]
    order += [(g, tail, 1) for g in (0, 1)] + [(g, h, 2) for h in range(tail) for g in (0, 1)]
    order += [(g, tail, 2) for g in (0, 1)] + [(g, h, 3) for g in (1 - y_lo, y_lo) for h in (tail, *range(tail))]
    for g, h, t in order:
        if t == 0:
            with scope(f"swap{g}"):
                swaps[g].wait_recv()
            result[g, :, :, both:] = result[g, :, :, both:] + swap_in[g].astype(F32)
        for d in (UP, DOWN):
            if t < STEPS[h][d]:
                sum_step(g, h, d, t)
    ends = []
    for far_rows, g in ((True, 1 - y_lo), (False, y_lo)):
        for h in (tail, *range(tail)):
            value = own_sum(g, h, z)
            for d in (UP, DOWN):
                last = STEPS[h][d] - 1
                with scope(f"rs{last}{h}{d}{far_rows}"):
                    sum_copy(g, h, d, last).wait_recv()
                value += arrived(g, h, d, last)
            there = final.at[g, :, spans[h]]
            final[g, :, spans[h]] = value.astype(BF16)
            columns = columns_of(y_lo, starts[h], WIDTHS[h])
            if far_rows:
                go(remote(there, out_ref.at[:, columns], send_sem.at[END], end_recv.at[0], across))
            else:
                ends.append(pltpu.make_async_copy(there, out_ref.at[:, columns], local_sem.at[h]))
                ends[-1].start()
    with scope("ends"):
        got_all(final.at[0], end_recv.at[0])
        for copy in ends:
            copy.wait()
    with scope("drain"):
        sent_all(final.at[0], send_sem.at[END])
        sent_all(bands.at[:, pl.ds(0, Z - 1)], send_sem.at[RING])
        sent_all(away, send_sem.at[ACROSS])
        sent_all(proj.at[0, 0, :, pl.ds(0, both)], send_sem.at[PIECE_SEND])
        sent_all(proj.at[0, 0], send_sem.at[MATE])
        sent_all(coefs.at[pl.ds(0, 3)], send_sem.at[COEFS])
        sent_all(proj.at[0, 0, :, pl.ds(0, both)], send_sem.at[PASS])
        sent_all(parts, send_sem.at[PART])
        sent_all(weighted.at[:, pl.ds(0, PLANE - 1)], send_sem.at[WEIGHTED])
        sent_all(swap_out, send_sem.at[SWAP])
        sent_all(bands.at[:, pl.ds(0, Z - 1), :, pl.ds(0, half)], send_sem.at[SUM])


def shards(wave_rows, projectors, dij_table, dij_index, proj_count):
    rows, width = wave_rows.shape
    count = projectors.shape[0]
    half = width // 2
    wide = half + ALONE
    kinds, per_atom, _ = dij_table.shape
    atoms = count // per_atom

    dma = pltpu.SemaphoreType.DMA
    others = PLANE - 1
    hbm = pl.BlockSpec(memory_space=pltpu.MemorySpace.HBM)
    return pl.pallas_call(
        kernel,
        out_shape=jax.ShapeDtypeStruct((rows, width), BF16),
        in_specs=[hbm] * 5,
        out_specs=pl.BlockSpec(memory_space=pl.ANY),
        scratch_shapes=[
            pltpu.VMEM((2, Z, rows, wide), BF16),
            pltpu.VMEM((rows, wide), BF16),
            pltpu.VMEM((2, 2, count, wide), BF16),
            pltpu.VMEM((per_atom, per_atom, kinds), F32),
            pltpu.SMEM((atoms,), jnp.int32),
            pltpu.SMEM((atoms,), jnp.int32),
            pltpu.VMEM((4, per_atom, count), F32),
            pltpu.VMEM((2, PLANE, rows // 2, 4 * count), F32),
            pltpu.VMEM((2, others, rows // 2, 4 * count), F32),
            pltpu.VMEM((2, PLANE, rows // 2, 4 * count), BF16),
            pltpu.VMEM((2, Z, rows, half), F32),
            pltpu.VMEM((2, PARTS, Z - 1, rows, max(WIDTHS)), BF16),
            pltpu.VMEM((2, PARTS, Z - 1, rows, max(WIDTHS)), BF16),
            pltpu.VMEM((2, Z, rows, ALONE), BF16),
            pltpu.VMEM((2, Z, rows, ALONE), BF16),
            pltpu.VMEM((2, rows, half), BF16),
            pltpu.VMEM((4, count, count), F32),
            dma((SENDS,)),
            dma((2, 2, Z - 1)),
            dma((2,)),
            dma((1,)),
            dma((3,)),
            dma((4,)),
            dma((4,)),
            dma((2,)),
            dma((2,)),
            dma((2, PARTS, Z - 1)),
            dma((2,)),
            dma((1,)),
            dma((9,)),
        ],
        compiler_params=pltpu.CompilerParams(
            collective_id=0, has_side_effects=True, vmem_limit_bytes=67_043_328
        ),
        name="nonlocal_rows",
    )(wave_rows, projectors, jnp.transpose(dij_table, (1, 2, 0)), dij_index, proj_count)


def solution(mesh):
    return jax.shard_map(
        shards,
        mesh=mesh,
        in_specs=(P("atom", "band"), P("atom", "band"), P(), P("atom"), P("atom")),
        out_specs=P("atom", "band"),
        check_vma=False,
    )
```

time: 82 us -> 77.2 us (0.941)
  Pallas kernels: 80.2 us -> 75.4 us
    pallas_call x1, Pallas kernels: 80.2 us -> 75.4 us  [shards(): pl.pallas_call(kernel, out_shape=jax.ShapeDtypeStruct((rows, width), BF16...]
where the time goes in v3:
time: 77.2 us; the launch traced here: 77.1 us
  Pallas kernels  75.4 us (98%)
  local copies, waits for them, and re-layouts  1.67 us (2%)
    pallas_call x1, Pallas kernels, shards(): pl.pallas_call(kernel, out_shape=jax.ShapeDtypeStruct((rows, width), BF16...  75.4 us
    unnamed x1, local copies, waits for them, and re-layouts  1.67 us

profile of v3, /device:TPU:8, one launch (start us, length us, event | category | flops | bytes accessed | tf_op | source)
XLA Modules:
  0.0 77.1 jit_solution(10363757222259338330)
XLA Ops:
  0.0 75.4 %nonlocal_rows.1 = bf16[16,8192]{1,0:T(8,128)(2,1)} custom-call(bf16[16,8192]{1,0:T(8,128)(2,1)} %wave_ref.1, bf16[128,8192]{1,0:T(8,128)(2,1)} %proj_ref.1, f32[8,8,16]{2,1,0:T(8,128)} %bitcast.1, s32[16]{0:T(128)} %index_ref.1, s32[16]{0:T(128)} %count_ref.1), custom_call_target="tpu_custom_call" | custom-call | tf_op jit(solution)/shard_map/nonlocal_rows/pallas_call | solution.py:389
  75.4 1.7 %copy.7 = bf16[16,8192]{1,0:T(8,128)(2,1)} copy(bf16[16,8192]{1,0:T(8,128)(2,1)} %nonlocal_rows.1) | data formatting | bytes 524288

commit v4 on v3

v4 whole, which is shorter than its diff:
```python
import functools

import jax
import jax.numpy as jnp
from jax import lax
from jax.experimental import pallas as pl
from jax.experimental.pallas import tpu as pltpu
from jax.sharding import PartitionSpec as P

MESH = pl.DeviceIdType.MESH
F32 = jnp.float32
BF16 = jnp.bfloat16
scope = jax.named_scope
Z = 8
SIDE = 4
PLANE = SIDE * SIDE
PARTS = 4
PIECES = (1024, 1024, 1024, 768, 256)
UP, DOWN = 0, 1
RING, ACROSS, PIECE_SEND, MATE, COEFS, PASS, PART, WEIGHTED, SUM, END = range(10)
SENDS = 10
STEPS = ((4, 3), (3, 4), (4, 3), (3, 4))


def kernel(
    wave_ref, proj_ref, table_ref, index_ref, count_ref, out_ref,
    bands, away, proj, table, index, acting, coefs, part, parts, weighted, result, sent, came, last, across_share, final, mix,
    send_sem, ring_recv, y_recv, mate_recv, c_recv, piece_recv, pass_recv, part_recv, wt_recv, sum_recv, last_recv, end_recv,
    local_sem,
):
    rows, half = away.shape
    count = proj.shape[2]
    per_atom, _, kinds = table.shape
    share = rows // 2
    atom, band = lax.axis_index("atom"), lax.axis_index("band")
    y_lo, z, core = atom // (2 * Z), (atom // 2) % Z, atom % 2
    y_hi, x = band // SIDE, band % SIDE
    y = y_hi * 2 + y_lo
    me = y * SIDE + x
    slot = y_lo * 2 + core

    def at(lo, zz, cc, hi=y_hi, xx=x):
        return (lo * (2 * Z) + zz * 2 + cc, hi * SIDE + xx)

    mate = at(y_lo, z, 1 - core)
    across = at(1 - y_lo, z, core)
    corner = at(1 - y_lo, z, 1 - core)
    z_next = (at(y_lo, (z + 1) % Z, core), at(y_lo, (z + Z - 1) % Z, core))
    shifts = [(dy, dx) for dy in range(SIDE) for dx in range(SIDE) if dy or dx]
    shifts.sort(key=lambda s: -min(s[0], SIDE - s[0]) - min(s[1], SIDE - s[1]))

    def plane(dy, dx):
        yy, xx = (y + dy) % SIDE, (x + dx) % SIDE
        return yy * SIDE + xx, at(yy % 2, z, core, yy // 2, xx)

    def remote(src, dst, send, recv, to):
        return pltpu.make_async_remote_copy(
            src_ref=src, dst_ref=dst, send_sem=send, recv_sem=recv, device_id=to, device_id_type=MESH
        )

    def columns_of(side, first, size):
        return pl.ds(pl.multiple_of(side * half + first, 128), size)

    mine, theirs = columns_of(y_lo, 0, half), columns_of(1 - y_lo, 0, half)
    away_bands = pltpu.make_async_copy(wave_ref.at[:, theirs], away, local_sem.at[0])
    own_bands = pltpu.make_async_copy(wave_ref.at[:, mine], bands.at[y_lo, z], local_sem.at[1])
    own_proj = pltpu.make_async_copy(proj_ref.at[:, mine], proj.at[y_lo, core], local_sem.at[2])
    small = [
        pltpu.make_async_copy(table_ref, table, local_sem.at[3]),
        pltpu.make_async_copy(index_ref, index, local_sem.at[4]),
        pltpu.make_async_copy(count_ref, acting, local_sem.at[5]),
    ]
    for copy in (away_bands, own_bands, own_proj, *small):
        copy.start()

    barrier = pltpu.get_barrier_semaphore()
    slant = (at(1 - y_lo, (z + 1) % Z, core), at(1 - y_lo, (z + Z - 1) % Z, core))
    greet = [mate, corner, *z_next, *slant] + [plane(*s)[1] for s in shifts]
    for to in greet:
        pl.semaphore_signal(barrier, inc=1, device_id=to, device_id_type=MESH)
    with scope("barrier"):
        pl.semaphore_wait(barrier, len(greet))

    def go(copy):
        copy.start()
        return copy

    def sent_all(ref, sem):
        remote(ref, ref, sem, sem, mate).wait_send()

    def got_all(ref, sem):
        remote(ref, ref, sem, sem, mate).wait_recv()

    def ring_copy(k, h, d, t):
        source = (z + Z - t) % Z if d == UP else (z + t) % Z
        block = bands.at[y_lo if k == 0 else 1 - y_lo, source, :, pl.ds(h * (half // 2), half // 2)]
        return remote(block, block, send_sem.at[RING], ring_recv.at[k, h, d * STEPS[h][UP] + t], z_next[d])

    away_bands.wait()
    y_bands = []
    for h in (0, 1):
        columns = pl.ds(h * (half // 2), half // 2)
        y_bands.append(
            go(remote(away.at[:, columns], bands.at[y_lo, z, :, columns], send_sem.at[ACROSS], y_recv.at[h], across))
        )
    own_bands.wait()
    for h in (0, 1):
        for d in (UP, DOWN):
            go(ring_copy(0, h, d, 0))
    cuts = [(sum(PIECES[:i]), size) for i, size in enumerate(PIECES)]
    pieces = [
        remote(
            proj_ref.at[:, columns_of(1 - y_lo, first, size)], proj.at[y_lo, core, :, pl.ds(first, size)],
            send_sem.at[PIECE_SEND], piece_recv.at[i], across,
        )
        for i, (first, size) in enumerate(cuts)
    ]
    for copy in pieces[:2]:
        go(copy)
    own_proj.wait()
    there = proj.at[y_lo, core]
    to_mate = go(remote(there, there, send_sem.at[MATE], mate_recv.at[0], mate))

    for copy in small:
        copy.wait()
    flat = (per_atom, count)
    lane = lax.broadcasted_iota(jnp.int32, flat, 1)
    inner = lane % per_atom
    chosen = jnp.zeros(flat, jnp.int32)
    limit = jnp.zeros(flat, jnp.int32)
    for a in range(count // per_atom):
        chosen = jnp.where(lane // per_atom == a, index[a], chosen)
        limit = jnp.where(lane // per_atom == a, acting[a], limit)
    kind = lax.broadcasted_iota(jnp.int32, (kinds, count), 0)
    value = jnp.zeros(flat, F32)
    for i in range(per_atom):
        pick = jnp.where((kind == chosen[:1]) & (inner[:1] == i), 1.0, 0.0).astype(F32)
        value += jnp.dot(table[i], pick, precision=lax.Precision.HIGHEST, preferred_element_type=F32)
    on = (inner < limit) & (lax.broadcasted_iota(jnp.int32, flat, 0) < limit)
    coefs[slot] = jnp.where(on, value, 0.0)

    coef_copies = [
        go(remote(coefs.at[slot], coefs.at[slot], send_sem.at[COEFS], c_recv.at[i], to))
        for i, to in enumerate((mate, across, corner))
    ]
    for copy in pieces[2:]:
        go(copy)
    for h in (0, 1):
        with scope(f"ybands{h}"):
            y_bands[h].wait_recv()
        for d in (UP, DOWN):
            go(ring_copy(1, h, d, 0))
    passed = []

    def pass_piece(i):
        with scope(f"piece{i}"):
            pieces[i].wait_recv()
        first, size = cuts[i]
        there = proj.at[1 - y_lo, core, :, pl.ds(first, size)]
        passed.append(go(remote(there, there, send_sem.at[PASS], pass_recv.at[i], mate)))

    def contract(lines, kept):
        return lax.dot_general(lines, kept, (((1,), (1,)), ((), ())), preferred_element_type=F32)

    own_pair = pl.ds(pl.multiple_of(y_lo * 2 * count, count), 2 * count)
    far_pair = pl.ds(pl.multiple_of((1 - y_lo) * 2 * count, count), 2 * count)

    def own_parts(sources):
        lines = [bands[:, source].reshape(2 * rows, half) for source in sources]
        kept = proj[y_lo].reshape(2 * count, half)
        value = contract(kept, lines[0]).T if len(lines) == 1 else contract(jnp.concatenate(lines, axis=0), kept)
        for i, source in enumerate(sources):
            here = value[i * 2 * rows : (i + 1) * 2 * rows].reshape(2, 2, share, 2 * count)
            part[:, pl.ds(source * 2, 2), :, own_pair] = here

    def send_parts(g, columns):
        for i, s in enumerate(shifts):
            chunk, to = plane(*s)
            go(
                remote(
                    part.at[g, chunk, :, columns], parts.at[g, i, :, columns], send_sem.at[PART], part_recv.at[g], to
                )
            )

    for t in range(4):
        for k in (0, 1):
            for h in (0, 1):
                for d in (UP, DOWN):
                    if t < STEPS[h][d]:
                        with scope(f"ag{t}{k}{h}{d}"):
                            ring_copy(k, h, d, t).wait_recv()
                        if t + 1 < STEPS[h][d]:
                            go(ring_copy(k, h, d, t + 1))
        if t == 1:
            pass_piece(0)
            with scope("tomate"):
                to_mate.wait_recv()
            with scope("S1"):
                own_parts([(z + Z + i) % Z for i in range(-2, 3)])
        if t == 2:
            pass_piece(1)
            with scope("S2"):
                own_parts([(z + Z - 3) % Z, (z + 3) % Z])
            pass_piece(2)
    with scope("S3"):
        own_parts([(z + 4) % Z])
    send_parts(0, own_pair)

    every = 2 * Z * rows
    ready = cuts[3][0]
    with scope("passed0"):
        for copy in passed:
            copy.wait_recv()
    with scope("Sfar0"):
        value = contract(
            bands[:, :, :, :ready].reshape(every, ready), proj[1 - y_lo, :, :, :ready].reshape(2 * count, ready)
        )
        part[:, :, :, far_pair] = value.reshape(2, PLANE, share, 2 * count)
    pass_piece(3)
    pass_piece(4)
    with scope("mixes"):
        for copy in coef_copies:
            copy.wait_recv()
        square = (count, count)
        down = lax.broadcasted_iota(jnp.int32, square, 0)
        same = down // per_atom == lax.broadcasted_iota(jnp.int32, square, 1) // per_atom
        for s in range(4):
            mix[s] = jnp.where(same, jnp.concatenate([coefs[s]] * (count // per_atom), axis=0), 0.0)
    with scope("passed"):
        for copy in passed[3:]:
            copy.wait_recv()
    with scope("Sfar1"):
        value = contract(
            bands[:, :, :, ready:].reshape(every, half - ready),
            proj[1 - y_lo, :, :, ready:].reshape(2 * count, half - ready),
        )
        part[:, :, :, far_pair] += value.reshape(2, PLANE, share, 2 * count)
    send_parts(0, far_pair)
    send_parts(1, own_pair)
    send_parts(1, far_pair)
    for g in (0, 1):
        with scope(f"part{g}"):
            got_all(parts.at[g], part_recv.at[g])
        with scope(f"mix{g}"):
            total = part[g, me]
            for i in range(len(shifts)):
                total += parts[g, i]
            mixed = [
                jnp.dot(
                    total[:, s * count : (s + 1) * count], mix[s],
                    precision=lax.Precision.HIGHEST, preferred_element_type=F32,
                )
                for s in range(4)
            ]
            weighted[g, me] = jnp.concatenate(mixed, axis=1).astype(BF16)
        for i, s in enumerate(shifts):
            _, to = plane(*s)
            there = weighted.at[g, me]
            go(remote(there, there, send_sem.at[WEIGHTED], wt_recv.at[g], to))

    group = Z * rows
    tile = 512
    width = half // PARTS
    spans = [slice(h * width, (h + 1) * width) for h in range(PARTS)]

    def own_sum(g, h, owner):
        return result[g, owner, :, spans[h]]

    def at_step(h, d, t):
        return d * STEPS[h][UP] + t

    def sum_copy(g, h, d, t):
        n = at_step(h, d, t)
        if t < STEPS[h][d] - 1:
            return remote(
                sent.at[g, h, n], came.at[g, h, n], send_sem.at[SUM], sum_recv.at[g, h, n - d], z_next[d]
            )
        owner = at(g, (z + 1) % Z if d == UP else (z + Z - 1) % Z, core)
        return remote(sent.at[g, h, n], last.at[y_lo, h, d], send_sem.at[SUM], last_recv.at[y_lo, h, d], owner)

    def arrived(g, h, d, t):
        return came[g, h, at_step(h, d, t)].astype(F32)

    def sum_step(g, h, d, t):
        n = STEPS[h][d]
        owner = (z + (n - t)) % Z if d == UP else (z + Z - (n - t)) % Z
        value = own_sum(g, h, owner)
        if t > 0:
            with scope(f"rs{t - 1}{h}{d}"):
                sum_copy(g, h, d, t - 1).wait_recv()
            value += arrived(g, h, d, t - 1)
        sent[g, h, at_step(h, d, t)] = value.astype(BF16)
        go(sum_copy(g, h, d, t))

    for g in (0, 1):
        with scope(f"wt{g}"):
            got_all(weighted.at[g, pl.ds(0, PLANE - 1)], wt_recv.at[g])
        for h in range(PARTS):
            with scope(f"O{g}{h}"):
                for first in range(spans[h].start, spans[h].stop, tile):
                    size = min(tile, spans[h].stop - first)
                    value = jnp.dot(
                        weighted[g].reshape(group, 4 * count),
                        proj[:, :, :, first : first + size].reshape(4 * count, size),
                        preferred_element_type=F32,
                    )
                    result[g, :, :, first : first + size] = value.reshape(Z, rows, size)
            for d in (UP, DOWN):
                sum_step(g, h, d, 0)
    final[1 - y_lo] = result[1 - y_lo, z].astype(BF16)
    own_share = go(remote(final.at[1 - y_lo], across_share, send_sem.at[END], end_recv.at[0], across))
    order = [(g, h, t) for t in (1, 2, 3) for g in (0, 1) for h in range(PARTS)]
    for g, h, t in order:
        for d in (UP, DOWN):
            if t < STEPS[h][d]:
                sum_step(g, h, d, t)
    with scope("share"):
        own_share.wait_recv()
        sent_all(final.at[0], send_sem.at[END])
    ends = []
    for h in range(PARTS):
        for side, value in ((y_lo, result[y_lo, z, :, spans[h]]), (1 - y_lo, across_share[:, spans[h]].astype(F32))):
            for d in (UP, DOWN):
                here = last.at[side, h, d]
                with scope(f"last{h}{d}"):
                    remote(here, here, send_sem.at[SUM], last_recv.at[side, h, d], mate).wait_recv()
                value += last[side, h, d].astype(F32)
            final[side, :, spans[h]] = value.astype(BF16)
            ends.append(
                pltpu.make_async_copy(
                    final.at[side, :, spans[h]], out_ref.at[:, columns_of(side, h * width, width)],
                    local_sem.at[2 * h + len(ends) % 2],
                )
            )
            ends[-1].start()
    with scope("ends"):
        for copy in ends:
            copy.wait()
    with scope("drain"):
        sent_all(bands.at[:, pl.ds(0, Z - 1)], send_sem.at[RING])
        sent_all(away, send_sem.at[ACROSS])
        sent_all(proj.at[0, 0], send_sem.at[PIECE_SEND])
        sent_all(proj.at[0, 0], send_sem.at[MATE])
        sent_all(coefs.at[pl.ds(0, 3)], send_sem.at[COEFS])
        sent_all(proj.at[0, 0], send_sem.at[PASS])
        sent_all(parts, send_sem.at[PART])
        sent_all(weighted.at[:, pl.ds(0, PLANE - 1)], send_sem.at[WEIGHTED])
        sent_all(bands.at[:, pl.ds(0, Z - 1)], send_sem.at[SUM])


def shards(wave_rows, projectors, dij_table, dij_index, proj_count):
    rows, width = wave_rows.shape
    count = projectors.shape[0]
    half = width // 2
    kinds, per_atom, _ = dij_table.shape
    atoms = count // per_atom

    dma = pltpu.SemaphoreType.DMA
    others = PLANE - 1
    hbm = pl.BlockSpec(memory_space=pltpu.MemorySpace.HBM)
    return pl.pallas_call(
        kernel,
        out_shape=jax.ShapeDtypeStruct((rows, width), BF16),
        in_specs=[hbm] * 5,
        out_specs=pl.BlockSpec(memory_space=pl.ANY),
        scratch_shapes=[
            pltpu.VMEM((2, Z, rows, half), BF16),
            pltpu.VMEM((rows, half), BF16),
            pltpu.VMEM((2, 2, count, half), BF16),
            pltpu.VMEM((per_atom, per_atom, kinds), F32),
            pltpu.SMEM((atoms,), jnp.int32),
            pltpu.SMEM((atoms,), jnp.int32),
            pltpu.VMEM((4, per_atom, count), F32),
            pltpu.VMEM((2, PLANE, rows // 2, 4 * count), F32),
            pltpu.VMEM((2, others, rows // 2, 4 * count), F32),
            pltpu.VMEM((2, PLANE, rows // 2, 4 * count), BF16),
            pltpu.VMEM((2, Z, rows, half), F32),
            pltpu.VMEM((2, PARTS, Z - 1, rows, half // PARTS), BF16),
            pltpu.VMEM((2, PARTS, Z - 1, rows, half // PARTS), BF16),
            pltpu.VMEM((2, PARTS, 2, rows, half // PARTS), BF16),
            pltpu.VMEM((rows, half), BF16),
            pltpu.VMEM((2, rows, half), BF16),
            pltpu.VMEM((4, count, count), F32),
            dma((SENDS,)),
            dma((2, 2, Z - 1)),
            dma((2,)),
            dma((1,)),
            dma((3,)),
            dma((len(PIECES),)),
            dma((len(PIECES),)),
            dma((2,)),
            dma((2,)),
            dma((2, PARTS, Z - 3)),
            dma((2, PARTS, 2)),
            dma((1,)),
            dma((2 * PARTS,)),
        ],
        compiler_params=pltpu.CompilerParams(
            collective_id=0, has_side_effects=True, vmem_limit_bytes=67_043_328
        ),
        name="nonlocal_rows",
    )(wave_rows, projectors, jnp.transpose(dij_table, (1, 2, 0)), dij_index, proj_count)


def solution(mesh):
    return jax.shard_map(
        shards,
        mesh=mesh,
        in_specs=(P("atom", "band"), P("atom", "band"), P(), P("atom"), P("atom")),
        out_specs=P("atom", "band"),
        check_vma=False,
    )
```

time: 77.2 us -> 74.7 us (0.968)
  Pallas kernels: 75.4 us -> 72.9 us
    pallas_call x1, Pallas kernels: 75.4 us -> 72.9 us  [shards(): pl.pallas_call(kernel, out_shape=jax.ShapeDtypeStruct((rows, width), BF16...]
where the time goes in v4:
time: 74.7 us; the launch traced here: 74.6 us
  Pallas kernels  72.9 us (98%)
  local copies, waits for them, and re-layouts  1.67 us (2%)
    pallas_call x1, Pallas kernels, shards(): pl.pallas_call(kernel, out_shape=jax.ShapeDtypeStruct((rows, width), BF16...  72.9 us
    unnamed x1, local copies, waits for them, and re-layouts  1.67 us

profile of v4, /device:TPU:8, one launch (start us, length us, event | category | flops | bytes accessed | tf_op | source)
XLA Modules:
  0.0 74.6 jit_solution(8018940740897301597)
XLA Ops:
  0.0 72.9 %nonlocal_rows.1 = bf16[16,8192]{1,0:T(8,128)(2,1)} custom-call(bf16[16,8192]{1,0:T(8,128)(2,1)} %wave_ref.1, bf16[128,8192]{1,0:T(8,128)(2,1)} %proj_ref.1, f32[8,8,16]{2,1,0:T(8,128)} %bitcast.1, s32[16]{0:T(128)} %index_ref.1, s32[16]{0:T(128)} %count_ref.1), custom_call_target="tpu_custom_call" | custom-call | tf_op jit(solution)/shard_map/nonlocal_rows/pallas_call | solution.py:361
  72.9 1.7 %copy.7 = bf16[16,8192]{1,0:T(8,128)(2,1)} copy(bf16[16,8192]{1,0:T(8,128)(2,1)} %nonlocal_rows.1) | data formatting | bytes 524288

commit v5 on v4

--- a/solution.py
+++ b/solution.py
@@ -17,15 +17,15 @@
 PARTS = 4
 PIECES = (1024, 1024, 1024, 768, 256)
 UP, DOWN = 0, 1
-RING, ACROSS, PIECE_SEND, MATE, COEFS, PASS, PART, WEIGHTED, SUM, END = range(10)
-SENDS = 10
+RING, ACROSS, HAND, PIECE_SEND, MATE, COEFS, PASS, PART, WEIGHTED, SUM, END = range(11)
+SENDS = 11
 STEPS = ((4, 3), (3, 4), (4, 3), (3, 4))
 
 
 def kernel(
     wave_ref, proj_ref, table_ref, index_ref, count_ref, out_ref,
-    bands, away, proj, table, index, acting, coefs, part, parts, weighted, result, sent, came, last, across_share, final, mix,
-    send_sem, ring_recv, y_recv, mate_recv, c_recv, piece_recv, pass_recv, part_recv, wt_recv, sum_recv, last_recv, end_recv,
+    bands, away, stage, proj, table, index, acting, coefs, part, parts, weighted, result, sent, came, last, across_share, final, mix,
+    send_sem, ring_recv, y_recv, mate_recv, c_recv, hand_recv, piece_recv, pass_recv, part_recv, wt_recv, sum_recv, last_recv, end_recv,
     local_sem,
 ):
     rows, half = away.shape
@@ -108,15 +108,28 @@
         for d in (UP, DOWN):
             go(ring_copy(0, h, d, 0))
     cuts = [(sum(PIECES[:i]), size) for i, size in enumerate(PIECES)]
+    hand = remote(proj_ref.at[:, theirs], stage, send_sem.at[HAND], hand_recv.at[0], mate)
     pieces = [
-        remote(
-            proj_ref.at[:, columns_of(1 - y_lo, first, size)], proj.at[y_lo, core, :, pl.ds(first, size)],
-            send_sem.at[PIECE_SEND], piece_recv.at[i], across,
-        )
+        [
+            remote(
+                source, proj.at[y_lo, c, :, pl.ds(first, size)], send_sem.at[PIECE_SEND], piece_recv.at[c, i], across
+            )
+            for c, source in (
+                (0, stage.at[:, pl.ds(first, size)]), (1, proj_ref.at[:, columns_of(1 - y_lo, first, size)])
+            )
+        ]
         for i, (first, size) in enumerate(cuts)
     ]
-    for copy in pieces[:2]:
-        go(copy)
+
+    @pl.when(core == 0)
+    def _():
+        hand.start()
+
+    @pl.when(core == 1)
+    def _():
+        for i in (0, 1):
+            pieces[i][1].start()
+
     own_proj.wait()
     there = proj.at[y_lo, core]
     to_mate = go(remote(there, there, send_sem.at[MATE], mate_recv.at[0], mate))
@@ -143,21 +156,39 @@
         go(remote(coefs.at[slot], coefs.at[slot], send_sem.at[COEFS], c_recv.at[i], to))
         for i, to in enumerate((mate, across, corner))
     ]
-    for copy in pieces[2:]:
-        go(copy)
     for h in (0, 1):
         with scope(f"ybands{h}"):
             y_bands[h].wait_recv()
         for d in (UP, DOWN):
             go(ring_copy(1, h, d, 0))
-    passed = []
+
+    @pl.when(core == 1)
+    def _():
+        hand.wait_recv()
+        for i in (0, 1):
+            pieces[i][0].start()
+        for pair in pieces[2:]:
+            for copy in pair:
+                copy.start()
+
+    def passing(i):
+        first, size = cuts[i]
+        there = proj.at[1 - y_lo, :, :, pl.ds(first, size)]
+        return remote(there, there, send_sem.at[PASS], pass_recv.at[i], mate)
 
     def pass_piece(i):
-        with scope(f"piece{i}"):
-            pieces[i].wait_recv()
-        first, size = cuts[i]
-        there = proj.at[1 - y_lo, core, :, pl.ds(first, size)]
-        passed.append(go(remote(there, there, send_sem.at[PASS], pass_recv.at[i], mate)))
+        @pl.when(core == 1)
+        def _():
+            with scope(f"piece{i}"):
+                for copy in pieces[i]:
+                    copy.wait_recv()
+            passing(i).start()
+
+    def take_piece(i):
+        @pl.when(core == 0)
+        def _():
+            with scope(f"take{i}"):
+                passing(i).wait_recv()
 
     def contract(lines, kept):
         return lax.dot_general(lines, kept, (((1,), (1,)), ((), ())), preferred_element_type=F32)
@@ -204,19 +235,22 @@
             pass_piece(2)
     with scope("S3"):
         own_parts([(z + 4) % Z])
-    send_parts(0, own_pair)
-
     every = 2 * Z * rows
-    ready = cuts[3][0]
-    with scope("passed0"):
-        for copy in passed:
-            copy.wait_recv()
+
+    def far_parts(first, size):
+        return contract(
+            bands[:, :, :, first : first + size].reshape(every, size),
+            proj[1 - y_lo, :, :, first : first + size].reshape(2 * count, size),
+        ).reshape(2, PLANE, share, 2 * count)
+
+    for i in range(3):
+        take_piece(i)
     with scope("Sfar0"):
-        value = contract(
-            bands[:, :, :, :ready].reshape(every, ready), proj[1 - y_lo, :, :, :ready].reshape(2 * count, ready)
-        )
-        part[:, :, :, far_pair] = value.reshape(2, PLANE, share, 2 * count)
+        part[:, :, :, far_pair] = far_parts(0, cuts[3][0])
     pass_piece(3)
+    take_piece(3)
+    with scope("Sfar1"):
+        part[:, :, :, far_pair] += far_parts(*cuts[3])
     pass_piece(4)
     with scope("mixes"):
         for copy in coef_copies:
@@ -226,18 +260,11 @@
         same = down // per_atom == lax.broadcasted_iota(jnp.int32, square, 1) // per_atom
         for s in range(4):
             mix[s] = jnp.where(same, jnp.concatenate([coefs[s]] * (count // per_atom), axis=0), 0.0)
-    with scope("passed"):
-        for copy in passed[3:]:
-            copy.wait_recv()
-    with scope("Sfar1"):
-        value = contract(
-            bands[:, :, :, ready:].reshape(every, half - ready),
-            proj[1 - y_lo, :, :, ready:].reshape(2 * count, half - ready),
-        )
-        part[:, :, :, far_pair] += value.reshape(2, PLANE, share, 2 * count)
-    send_parts(0, far_pair)
-    send_parts(1, own_pair)
-    send_parts(1, far_pair)
+    take_piece(4)
+    with scope("Sfar2"):
+        part[:, :, :, far_pair] += far_parts(*cuts[4])
+    for g in (0, 1):
+        send_parts(g, slice(None))
     for g in (0, 1):
         with scope(f"part{g}"):
             got_all(parts.at[g], part_recv.at[g])
@@ -339,10 +366,18 @@
     with scope("drain"):
         sent_all(bands.at[:, pl.ds(0, Z - 1)], send_sem.at[RING])
         sent_all(away, send_sem.at[ACROSS])
-        sent_all(proj.at[0, 0], send_sem.at[PIECE_SEND])
         sent_all(proj.at[0, 0], send_sem.at[MATE])
         sent_all(coefs.at[pl.ds(0, 3)], send_sem.at[COEFS])
-        sent_all(proj.at[0, 0], send_sem.at[PASS])
+
+        @pl.when(core == 0)
+        def _():
+            sent_all(stage, send_sem.at[HAND])
+
+        @pl.when(core == 1)
+        def _():
+            sent_all(proj.at[0], send_sem.at[PIECE_SEND])
+            sent_all(proj.at[0], send_sem.at[PASS])
+
         sent_all(parts, send_sem.at[PART])
         sent_all(weighted.at[:, pl.ds(0, PLANE - 1)], send_sem.at[WEIGHTED])
         sent_all(bands.at[:, pl.ds(0, Z - 1)], send_sem.at[SUM])
@@ -366,6 +401,7 @@
         scratch_shapes=[
             pltpu.VMEM((2, Z, rows, half), BF16),
             pltpu.VMEM((rows, half), BF16),
+            pltpu.VMEM((count, half), BF16),
             pltpu.VMEM((2, 2, count, half), BF16),
             pltpu.VMEM((per_atom, per_atom, kinds), F32),
             pltpu.SMEM((atoms,), jnp.int32),
@@ -386,7 +422,8 @@
             dma((2,)),
             dma((1,)),
             dma((3,)),
-            dma((len(PIECES),)),
+            dma((1,)),
+            dma((2, len(PIECES))),
             dma((len(PIECES),)),
             dma((2,)),
             dma((2,)),

time: 74.7 us -> 74 us (level)
  no operation moved by 1% of the time
where the time goes in v5:
time: 74 us; the launch traced here: 73.9 us
  Pallas kernels  72.2 us (98%)
  local copies, waits for them, and re-layouts  1.67 us (2%)
    pallas_call x1, Pallas kernels, shards(): pl.pallas_call(kernel, out_shape=jax.ShapeDtypeStruct((rows, width), BF16...  72.2 us
    unnamed x1, local copies, waits for them, and re-layouts  1.67 us

profile of v5, /device:TPU:8, one launch (start us, length us, event | category | flops | bytes accessed | tf_op | source)
XLA Modules:
  0.0 73.9 jit_solution(11376819199288582387)
XLA Ops:
  0.0 72.2 %nonlocal_rows.1 = bf16[16,8192]{1,0:T(8,128)(2,1)} custom-call(bf16[16,8192]{1,0:T(8,128)(2,1)} %wave_ref.1, bf16[128,8192]{1,0:T(8,128)(2,1)} %proj_ref.1, f32[8,8,16]{2,1,0:T(8,128)} %bitcast.1, s32[16]{0:T(128)} %index_ref.1, s32[16]{0:T(128)} %count_ref.1), custom_call_target="tpu_custom_call" | custom-call | tf_op jit(solution)/shard_map/nonlocal_rows/pallas_call | solution.py:396
  72.2 1.7 %copy.7 = bf16[16,8192]{1,0:T(8,128)(2,1)} copy(bf16[16,8192]{1,0:T(8,128)(2,1)} %nonlocal_rows.1) | data formatting | bytes 524288

commit v6 on v5

--- a/solution.py
+++ b/solution.py
@@ -344,7 +344,6 @@
     with scope("share"):
         own_share.wait_recv()
         sent_all(final.at[0], send_sem.at[END])
-    ends = []
     for h in range(PARTS):
         for side, value in ((y_lo, result[y_lo, z, :, spans[h]]), (1 - y_lo, across_share[:, spans[h]].astype(F32))):
             for d in (UP, DOWN):
@@ -352,17 +351,7 @@
                 with scope(f"last{h}{d}"):
                     remote(here, here, send_sem.at[SUM], last_recv.at[side, h, d], mate).wait_recv()
                 value += last[side, h, d].astype(F32)
-            final[side, :, spans[h]] = value.astype(BF16)
-            ends.append(
-                pltpu.make_async_copy(
-                    final.at[side, :, spans[h]], out_ref.at[:, columns_of(side, h * width, width)],
-                    local_sem.at[2 * h + len(ends) % 2],
-                )
-            )
-            ends[-1].start()
-    with scope("ends"):
-        for copy in ends:
-            copy.wait()
+            out_ref[:, columns_of(side, h * width, width)] = value.astype(BF16)
     with scope("drain"):
         sent_all(bands.at[:, pl.ds(0, Z - 1)], send_sem.at[RING])
         sent_all(away, send_sem.at[ACROSS])
@@ -393,11 +382,15 @@
     dma = pltpu.SemaphoreType.DMA
     others = PLANE - 1
     hbm = pl.BlockSpec(memory_space=pltpu.MemorySpace.HBM)
+    operands = [
+        pltpu.with_memory_space_constraint(value, pltpu.MemorySpace.HBM)
+        for value in (wave_rows, projectors, jnp.transpose(dij_table, (1, 2, 0)), dij_index, proj_count)
+    ]
     return pl.pallas_call(
         kernel,
         out_shape=jax.ShapeDtypeStruct((rows, width), BF16),
         in_specs=[hbm] * 5,
-        out_specs=pl.BlockSpec(memory_space=pl.ANY),
+        out_specs=pl.BlockSpec(memory_space=pltpu.MemorySpace.VMEM),
         scratch_shapes=[
             pltpu.VMEM((2, Z, rows, half), BF16),
             pltpu.VMEM((rows, half), BF16),
@@ -433,10 +426,10 @@
             dma((2 * PARTS,)),
         ],
         compiler_params=pltpu.CompilerParams(
-            collective_id=0, has_side_effects=True, vmem_limit_bytes=67_043_328
+            collective_id=0, has_side_effects=True, vmem_limit_bytes=40 * 1024 * 1024
         ),
         name="nonlocal_rows",
-    )(wave_rows, projectors, jnp.transpose(dij_table, (1, 2, 0)), dij_index, proj_count)
+    )(*operands)
 
 
 def solution(mesh):

time: 74 us -> 72.4 us (0.978)
  local copies, waits for them, and re-layouts: 1.67 us -> 0.71 us
    unnamed x1, local copies, waits for them, and re-layouts: 1.67 us -> 0.71 us
where the time goes in v6:
time: 72.4 us; the launch traced here: 72.3 us
  Pallas kernels  71.6 us (99%)
    pallas_call x1, Pallas kernels, shards(): pl.pallas_call(kernel, out_shape=jax.ShapeDtypeStruct((rows, width), BF16...  71.6 us

profile of v6, /device:TPU:8, one launch (start us, length us, event | category | flops | bytes accessed | tf_op | source)
XLA Modules:
  0.0 72.3 jit_solution(15317349698651098831)
XLA Ops:
  0.0 71.6 %nonlocal_rows.1 = bf16[16,8192]{1,0:T(8,128)(2,1)S(1)} custom-call(bf16[16,8192]{1,0:T(8,128)(2,1)} %wave_ref.1, bf16[128,8192]{1,0:T(8,128)(2,1)} %proj_ref.1, f32[8,8,16]{2,1,0:T(8,128)} %bitcast.1, s32[16]{0:T(128)} %index_ref.1, s32[16]{0:T(128)} %count_ref.1), custom_call_target="tpu_custom_call" | custom-call | tf_op jit(solution)/shard_map/nonlocal_rows/pallas_call | solution.py:389
  71.6 0.7 copy.7

commit v7 on v6

--- a/solution.py
+++ b/solution.py
@@ -15,7 +15,7 @@
 SIDE = 4
 PLANE = SIDE * SIDE
 PARTS = 4
-PIECES = (1024, 1024, 1024, 768, 256)
+PIECES = (1024, 1024, 1024, 896, 128)
 UP, DOWN = 0, 1
 RING, ACROSS, HAND, PIECE_SEND, MATE, COEFS, PASS, PART, WEIGHTED, SUM, END = range(11)
 SENDS = 11
@@ -47,7 +47,7 @@
     corner = at(1 - y_lo, z, 1 - core)
     z_next = (at(y_lo, (z + 1) % Z, core), at(y_lo, (z + Z - 1) % Z, core))
     shifts = [(dy, dx) for dy in range(SIDE) for dx in range(SIDE) if dy or dx]
-    shifts.sort(key=lambda s: -min(s[0], SIDE - s[0]) - min(s[1], SIDE - s[1]))
+    shifts.sort(key=lambda s: -2 * min(s[0], SIDE - s[0]) - min(s[1], SIDE - s[1]))
 
     def plane(dy, dx):
         yy, xx = (y + dy) % SIDE, (x + dx) % SIDE
@@ -255,11 +255,12 @@
     with scope("mixes"):
         for copy in coef_copies:
             copy.wait_recv()
-        square = (count, count)
-        down = lax.broadcasted_iota(jnp.int32, square, 0)
-        same = down // per_atom == lax.broadcasted_iota(jnp.int32, square, 1) // per_atom
+        down = lax.broadcasted_iota(jnp.int32, flat, 0)
         for s in range(4):
-            mix[s] = jnp.where(same, jnp.concatenate([coefs[s]] * (count // per_atom), axis=0), 0.0)
+            for d in range(2 * per_atom - 1):
+                mix[s, d] = jnp.sum(
+                    jnp.where(down == inner + d - (per_atom - 1), coefs[s], 0.0), axis=0, keepdims=True
+                )
     take_piece(4)
     with scope("Sfar2"):
         part[:, :, :, far_pair] += far_parts(*cuts[4])
@@ -272,13 +273,14 @@
             total = part[g, me]
             for i in range(len(shifts)):
                 total += parts[g, i]
-            mixed = [
-                jnp.dot(
-                    total[:, s * count : (s + 1) * count], mix[s],
-                    precision=lax.Precision.HIGHEST, preferred_element_type=F32,
-                )
-                for s in range(4)
-            ]
+            mixed = []
+            for s in range(4):
+                slot_total = total[:, s * count : (s + 1) * count]
+                value = slot_total * mix[s, per_atom - 1]
+                for d in range(2 * per_atom - 1):
+                    if d != per_atom - 1:
+                        value += pltpu.roll(slot_total, (count + per_atom - 1 - d) % count, 1) * mix[s, d]
+                mixed.append(value)
             weighted[g, me] = jnp.concatenate(mixed, axis=1).astype(BF16)
         for i, s in enumerate(shifts):
             _, to = plane(*s)
@@ -303,7 +305,7 @@
                 sent.at[g, h, n], came.at[g, h, n], send_sem.at[SUM], sum_recv.at[g, h, n - d], z_next[d]
             )
         owner = at(g, (z + 1) % Z if d == UP else (z + Z - 1) % Z, core)
-        return remote(sent.at[g, h, n], last.at[y_lo, h, d], send_sem.at[SUM], last_recv.at[y_lo, h, d], owner)
+        return remote(sent.at[g, h, n], last.at[y_lo, h, d], send_sem.at[SUM], last_recv.at[y_lo, h], owner)
 
     def arrived(g, h, d, t):
         return came[g, h, at_step(h, d, t)].astype(F32)
@@ -346,10 +348,9 @@
         sent_all(final.at[0], send_sem.at[END])
     for h in range(PARTS):
         for side, value in ((y_lo, result[y_lo, z, :, spans[h]]), (1 - y_lo, across_share[:, spans[h]].astype(F32))):
+            with scope(f"last{h}"):
+                got_all(last.at[side, h], last_recv.at[side, h])
             for d in (UP, DOWN):
-                here = last.at[side, h, d]
-                with scope(f"last{h}{d}"):
-                    remote(here, here, send_sem.at[SUM], last_recv.at[side, h, d], mate).wait_recv()
                 value += last[side, h, d].astype(F32)
             out_ref[:, columns_of(side, h * width, width)] = value.astype(BF16)
     with scope("drain"):
@@ -409,7 +410,7 @@
             pltpu.VMEM((2, PARTS, 2, rows, half // PARTS), BF16),
             pltpu.VMEM((rows, half), BF16),
             pltpu.VMEM((2, rows, half), BF16),
-            pltpu.VMEM((4, count, count), F32),
+            pltpu.VMEM((4, 2 * per_atom - 1, 1, count), F32),
             dma((SENDS,)),
             dma((2, 2, Z - 1)),
             dma((2,)),
@@ -421,7 +422,7 @@
             dma((2,)),
             dma((2,)),
             dma((2, PARTS, Z - 3)),
-            dma((2, PARTS, 2)),
+            dma((2, PARTS)),
             dma((1,)),
             dma((2 * PARTS,)),
         ],

time: 72.4 us -> 71.8 us (level)
  no operation moved by 1% of the time
where the time goes in v7:
time: 71.8 us; the launch traced here: 71.7 us
  Pallas kernels  71 us (99%)
    pallas_call x1, Pallas kernels, shards(): pl.pallas_call(kernel, out_shape=jax.ShapeDtypeStruct((rows, width), BF16...  71 us

profile of v7, /device:TPU:8, one launch (start us, length us, event | category | flops | bytes accessed | tf_op | source)
XLA Modules:
  0.0 71.7 jit_solution(11876870318969663271)
XLA Ops:
  0.0 71.0 %nonlocal_rows.1 = bf16[16,8192]{1,0:T(8,128)(2,1)S(1)} custom-call(bf16[16,8192]{1,0:T(8,128)(2,1)} %wave_ref.1, bf16[128,8192]{1,0:T(8,128)(2,1)} %proj_ref.1, f32[8,8,16]{2,1,0:T(8,128)} %bitcast.1, s32[16]{0:T(128)} %index_ref.1, s32[16]{0:T(128)} %count_ref.1), custom_call_target="tpu_custom_call" | custom-call | tf_op jit(solution)/shard_map/nonlocal_rows/pallas_call | solution.py:390
  71.0 0.7 copy.7

commit v8 on v7

--- a/solution.py
+++ b/solution.py
@@ -14,7 +14,7 @@
 Z = 8
 SIDE = 4
 PLANE = SIDE * SIDE
-PARTS = 4
+PARTS = 2
 PIECES = (1024, 1024, 1024, 896, 128)
 UP, DOWN = 0, 1
 RING, ACROSS, HAND, PIECE_SEND, MATE, COEFS, PASS, PART, WEIGHTED, SUM, END = range(11)
@@ -424,7 +424,7 @@
             dma((2, PARTS, Z - 3)),
             dma((2, PARTS)),
             dma((1,)),
-            dma((2 * PARTS,)),
+            dma((6,)),
         ],
         compiler_params=pltpu.CompilerParams(
             collective_id=0, has_side_effects=True, vmem_limit_bytes=40 * 1024 * 1024

time: 71.8 us -> 71.8 us (level)
  no operation moved by 1% of the time
where the time goes in v8:
time: 71.8 us; the launch traced here: 71.7 us
  Pallas kernels  71 us (99%)
    pallas_call x1, Pallas kernels, shards(): pl.pallas_call(kernel, out_shape=jax.ShapeDtypeStruct((rows, width), BF16...  71 us

profile of v8, /device:TPU:8, one launch (start us, length us, event | category | flops | bytes accessed | tf_op | source)
XLA Modules:
  0.0 71.7 jit_solution(3593939375545213027)
XLA Ops:
  0.0 71.0 %nonlocal_rows.1 = bf16[16,8192]{1,0:T(8,128)(2,1)S(1)} custom-call(bf16[16,8192]{1,0:T(8,128)(2,1)} %wave_ref.1, bf16[128,8192]{1,0:T(8,128)(2,1)} %proj_ref.1, f32[8,8,16]{2,1,0:T(8,128)} %bitcast.1, s32[16]{0:T(128)} %index_ref.1, s32[16]{0:T(128)} %count_ref.1), custom_call_target="tpu_custom_call" | custom-call | tf_op jit(solution)/shard_map/nonlocal_rows/pallas_call | solution.py:390
  71.0 0.7 copy.7

commit v9 on v8

--- a/solution.py
+++ b/solution.py
@@ -14,7 +14,7 @@
 Z = 8
 SIDE = 4
 PLANE = SIDE * SIDE
-PARTS = 2
+PARTS = 4
 PIECES = (1024, 1024, 1024, 896, 128)
 UP, DOWN = 0, 1
 RING, ACROSS, HAND, PIECE_SEND, MATE, COEFS, PASS, PART, WEIGHTED, SUM, END = range(11)
@@ -112,7 +112,7 @@
     pieces = [
         [
             remote(
-                source, proj.at[y_lo, c, :, pl.ds(first, size)], send_sem.at[PIECE_SEND], piece_recv.at[c, i], across
+                source, proj.at[y_lo, c, :, pl.ds(first, size)], send_sem.at[PIECE_SEND], piece_recv.at[i], across
             )
             for c, source in (
                 (0, stage.at[:, pl.ds(first, size)]), (1, proj_ref.at[:, columns_of(1 - y_lo, first, size)])
@@ -152,10 +152,8 @@
     on = (inner < limit) & (lax.broadcasted_iota(jnp.int32, flat, 0) < limit)
     coefs[slot] = jnp.where(on, value, 0.0)
 
-    coef_copies = [
-        go(remote(coefs.at[slot], coefs.at[slot], send_sem.at[COEFS], c_recv.at[i], to))
-        for i, to in enumerate((mate, across, corner))
-    ]
+    for to in (mate, across, corner):
+        go(remote(coefs.at[slot], coefs.at[slot], send_sem.at[COEFS], c_recv.at[0], to))
     for h in (0, 1):
         with scope(f"ybands{h}"):
             y_bands[h].wait_recv()
@@ -171,17 +169,19 @@
             for copy in pair:
                 copy.start()
 
+    def passed_block(i):
+        first, size = cuts[i]
+        return proj.at[1 - y_lo, :, :, pl.ds(first, size)]
+
     def passing(i):
-        first, size = cuts[i]
-        there = proj.at[1 - y_lo, :, :, pl.ds(first, size)]
+        there = passed_block(i)
         return remote(there, there, send_sem.at[PASS], pass_recv.at[i], mate)
 
     def pass_piece(i):
         @pl.when(core == 1)
         def _():
             with scope(f"piece{i}"):
-                for copy in pieces[i]:
-                    copy.wait_recv()
+                got_all(passed_block(i), piece_recv.at[i])
             passing(i).start()
 
     def take_piece(i):
@@ -253,8 +253,7 @@
         part[:, :, :, far_pair] += far_parts(*cuts[3])
     pass_piece(4)
     with scope("mixes"):
-        for copy in coef_copies:
-            copy.wait_recv()
+        got_all(coefs.at[pl.ds(0, 3)], c_recv.at[0])
         down = lax.broadcasted_iota(jnp.int32, flat, 0)
         for s in range(4):
             for d in range(2 * per_atom - 1):
@@ -415,9 +414,9 @@
             dma((2, 2, Z - 1)),
             dma((2,)),
             dma((1,)),
-            dma((3,)),
             dma((1,)),
-            dma((2, len(PIECES))),
+            dma((1,)),
+            dma((len(PIECES),)),
             dma((len(PIECES),)),
             dma((2,)),
             dma((2,)),

time: 71.8 us -> 71.7 us (level)
  no operation moved by 1% of the time
where the time goes in v9:
time: 71.7 us
  Pallas kernels  70.9 us (99%)
    pallas_call x1, Pallas kernels, shards(): pl.pallas_call(kernel, out_shape=jax.ShapeDtypeStruct((rows, width), BF16...  70.9 us

profile of v9, /device:TPU:8, one launch (start us, length us, event | category | flops | bytes accessed | tf_op | source)
XLA Modules:
  0.0 71.7 jit_solution(430958542614991438)
XLA Ops:
  0.0 70.9 %nonlocal_rows.1 = bf16[16,8192]{1,0:T(8,128)(2,1)S(1)} custom-call(bf16[16,8192]{1,0:T(8,128)(2,1)} %wave_ref.1, bf16[128,8192]{1,0:T(8,128)(2,1)} %proj_ref.1, f32[8,8,16]{2,1,0:T(8,128)} %bitcast.1, s32[16]{0:T(128)} %index_ref.1, s32[16]{0:T(128)} %count_ref.1), custom_call_target="tpu_custom_call" | custom-call | tf_op jit(solution)/shard_map/nonlocal_rows/pallas_call | solution.py:389
  71.0 0.7 copy.7
